TPU v7x, 32 devices: a whole 2x2x4 slice. The times are simulated.
32 devices in a mesh: tm: 4 (over y, core), space: 8 (over z, x).
Axes of the slice: x: 2, y: 2, z: 4, core: 2. Of those that a mesh axis runs over, the one named last changes fastest.
Arguments:
- perm_field: float32 [4, 32, 32, 256], P(None, 'space'), may hold values from 0.5 to 2
- step_multiplier: float32 [4, 32, 32, 256], P('tm', 'space'), may hold values from 0.5 to 2
- inflow: float32 [4, 32, 32, 256], P('tm', 'space'), may hold values from -3 to 3
- start_pressure: float32 [32, 32, 256], P('space'), may hold values from -6 to 6
- start_saturation: float32 [32, 32, 256], P('space'), may hold values from 0.1 to 0.9
- region_ids: int32 [32, 32, 256], P('space'), may hold values from 0 to 7
- region_table: float32 [3, 8], replicated, may hold values from 0.25 to 2
- well_cells: int32 [32], replicated, may hold values from 0 to 262143
- well_rates: float32 [4, 32], P('tm'), may hold values from -8 to 8
- observed: float32 [4, 4, 32], P(None, 'tm'), may hold values from -6 to 6
Outputs:
- misfit: float32 [4], replicated
- slab_pressure: float32 [4, 4, 32, 32, 256], P('tm', None, 'space')
- slab_saturation: float32 [4, 4, 32, 32, 256], P('tm', None, 'space')
All inputs are finite; a program needn't handle non-finite values.
Results may differ from a plain program's by a relative error of at most 0.0003.
Values sent between devices are 32-bit elements; how exact they have to be, the bound alone decides.
A program may use at most 64 MiB of HBM per device.

v0:
```python
import jax
import jax.numpy as jnp
from jax import lax
from jax.sharding import PartitionSpec as P

MB = 1
REP_DEV = 1
ITERS = 3


def padded(cells, sides, width):
    for axis, dim in sides:
        count = lax.axis_size(axis)
        ends = count - 1
        head = lax.slice_in_dim(cells, 0, width, axis=dim)
        tail = lax.slice_in_dim(cells, cells.shape[dim] - width, cells.shape[dim], axis=dim)
        cells = jnp.concatenate(
            [
                lax.ppermute(tail, axis, [(i, (i + 1) % count) for i in range(ends)]),
                cells,
                lax.ppermute(head, axis, [((i + 1) % count, i) for i in range(ends)]),
            ],
            axis=dim,
        )
    return cells


def shifted(values, dimension, offset):
    margins = [(0, 0)] * values.ndim
    length = values.shape[dimension]
    if offset > 0:
        margins[dimension] = (1, 0)
        return lax.slice_in_dim(jnp.pad(values, margins), 0, length, axis=dimension)
    margins[dimension] = (0, 1)
    return lax.slice_in_dim(jnp.pad(values, margins), 1, length + 1, axis=dimension)


def neighbour_values(values_ext):
    middle = values_ext[:, 1:-1]
    return (
        values_ext[:, :-2],
        values_ext[:, 2:],
        shifted(middle, 2, 1),
        shifted(middle, 2, -1),
        shifted(middle, 3, 1),
        shifted(middle, 3, -1),
    )


def coefficients(conduct_ext):
    middle = conduct_ext[:, 1:-1]
    others = neighbour_values(conduct_ext)
    links = [jnp.sqrt(middle * other_side) for other_side in others]
    link_total = links[0] + links[1] + links[2] + links[3] + links[4] + links[5]
    return tuple(links) + (link_total,)


def jacobi_sweep(pressure_ext, couplings, storage, right_side):
    beside = neighbour_values(pressure_ext)
    inflowing = couplings[0] * beside[0]
    for link_index in range(1, 6):
        inflowing = inflowing + couplings[link_index] * beside[link_index]
    divisor = jnp.where(storage > 0, storage + couplings[6], 1.0)
    return (right_side + inflowing) / divisor


def fraction(saturation, ratio):
    squared = saturation * saturation
    remain = (1.0 - saturation) * (1.0 - saturation)
    return squared / (squared + ratio * remain)


def transport(pressure_ext, flow_ext, couplings, saturation, gain, source):
    centre_p = pressure_ext[:, 1:-1]
    centre_f = flow_ext[:, 1:-1]
    other_p = neighbour_values(pressure_ext)
    other_f = neighbour_values(flow_ext)
    outflow = None
    for link_index in range(6):
        face_flux = couplings[link_index] * (centre_p - other_p[link_index])
        carried = face_flux * jnp.where(face_flux > 0, centre_f, other_f[link_index])
        outflow = carried if outflow is None else outflow + carried
    gained = (
        jnp.maximum(source, 0.0) * (1.0 - saturation)
        - jnp.maximum(-source, 0.0) * centre_f
        - outflow
    )
    return saturation + gain * gained


def region_fields(region_ids, region_table):
    fields = []
    for table_row in range(3):
        summed = jnp.zeros(region_ids.shape, jnp.float32)
        for region_index in range(region_table.shape[1]):
            summed = summed + jnp.where(
                region_ids == region_index, region_table[table_row, region_index], 0.0
            )
        fields.append(summed)
    return (fields[0], fields[1], 0.1 * fields[2])


def advance(pressure, saturation, conduct, source, inflow_now, storage, ratio, gain):
    right_side = storage * pressure + source + inflow_now
    flow_frac = fraction(saturation, ratio)
    edges = padded(jnp.stack([conduct, pressure]), (("space", 2),), 1)
    couplings = coefficients(edges[0])
    iterate_ext = edges[1]
    iterate = pressure
    for sweep_index in range(ITERS):
        if sweep_index > 0:
            iterate_ext = padded(iterate, (("space", 1),), 1)
        iterate = jacobi_sweep(iterate_ext, couplings, storage, right_side)
    both = padded(jnp.stack([iterate, flow_frac]), (("space", 2),), 1)
    saturation = transport(both[0], both[1], couplings, saturation, gain, source)
    return (iterate, saturation)


def body(
    perm_field,
    step_multiplier,
    inflow,
    start_pressure,
    start_saturation,
    region_ids,
    region_table,
    well_cells,
    well_rates,
    observed,
):
    sections = lax.axis_size("tm")
    section_index = lax.axis_index("tm")
    space_index = lax.axis_index("space")
    grid_shape = start_pressure.shape
    width_x, depth, across = grid_shape
    batch_size = MB
    storage, ratio, gain = region_fields(region_ids, region_table)
    layer_ids = lax.broadcasted_iota(jnp.int32, grid_shape, 0) + space_index * width_x
    cell_ids = (
        layer_ids * depth + lax.broadcasted_iota(jnp.int32, grid_shape, 1)
    ) * across + lax.broadcasted_iota(jnp.int32, grid_shape, 2)
    well_picks = (well_cells[:, None] == cell_ids.reshape(1, -1)).astype(jnp.float32)
    well_owned = jnp.sum(well_picks, axis=1)
    start_p = jnp.broadcast_to(start_pressure, (batch_size,) + grid_shape)
    start_s = jnp.broadcast_to(start_saturation, (batch_size,) + grid_shape)

    def mismatch(pressure, measured):
        predicted = jnp.dot(
            pressure.reshape(batch_size, -1), well_picks.T, precision=lax.Precision.HIGHEST
        )
        return jnp.sum(well_owned * (predicted - measured) ** 2, axis=1)

    misfit = jnp.zeros((perm_field.shape[0],), jnp.float32)
    fields = (
        lax.all_gather(step_multiplier, "tm", axis=0, tiled=True),
        lax.all_gather(inflow, "tm", axis=0, tiled=True),
        lax.all_gather(well_rates, "tm", axis=0, tiled=True),
    )
    measured_all = lax.all_to_all(observed, "tm", split_axis=0, concat_axis=1, tiled=True)
    perm_rows = lax.dynamic_slice_in_dim(perm_field, section_index * batch_size, batch_size, 0)
    rate_rows = fields[2]
    placed = jnp.dot(rate_rows, well_picks, precision=lax.Precision.HIGHEST)
    all_sources = placed.reshape((rate_rows.shape[0],) + grid_shape)
    zero_ends = jnp.zeros((sections, batch_size) + grid_shape, jnp.float32)

    def one_section(slab_index, state_tuple):
        pressure, saturation, ends_p, ends_s, errors = state_tuple
        position = slab_index * REP_DEV + 0
        multiplier = lax.dynamic_index_in_dim(fields[0], position, 0, keepdims=False)
        inflow_now = lax.dynamic_index_in_dim(fields[1], position, 0, keepdims=False)
        source = lax.dynamic_index_in_dim(all_sources, position, 0, keepdims=False)
        pressure, saturation = advance(
            pressure, saturation, perm_rows * multiplier, source, inflow_now, storage, ratio, gain
        )
        errors = errors + mismatch(
            pressure, lax.dynamic_index_in_dim(measured_all, position, 1, keepdims=False)
        )
        ends_p = lax.dynamic_update_index_in_dim(ends_p, pressure, slab_index, 0)
        ends_s = lax.dynamic_update_index_in_dim(ends_s, saturation, slab_index, 0)
        return (pressure, saturation, ends_p, ends_s, errors)

    result = lax.fori_loop(
        0,
        sections,
        one_section,
        (start_p, start_s, zero_ends, zero_ends, jnp.zeros((batch_size,), jnp.float32)),
    )
    slab_pressure, slab_saturation = (
        lax.all_to_all(result[2], "tm", split_axis=0, concat_axis=1, tiled=True),
        lax.all_to_all(result[3], "tm", split_axis=0, concat_axis=1, tiled=True),
    )
    misfit = lax.dynamic_update_slice_in_dim(misfit, result[4], section_index * batch_size, 0)
    totals = lax.psum(misfit, ("tm", "space"))
    return (totals / (sections * REP_DEV * well_cells.shape[0]), slab_pressure, slab_saturation)


def solution(mesh):
    return jax.shard_map(
        body,
        mesh=mesh,
        in_specs=(
            P(None, "space", None, None),
            P("tm", "space", None, None),
            P("tm", "space", None, None),
            P("space", None, None),
            P("space", None, None),
            P("space", None, None),
            P(),
            P(),
            P("tm", None),
            P(None, "tm", None),
        ),
        out_specs=(P(), P("tm", None, "space", None, None), P("tm", None, "space", None, None)),
        check_vma=False,
    )
```

profile of v0, /device:TPU:0, one launch (start us, length us, event | category | flops | bytes accessed | tf_op | source)
XLA Modules:
  0.0 281.1 jit_solution(10147886916045654952)
XLA Ops:
  0.7 4.4 %all-to-all-start = ((f32[4,1,32]{2,1,0:T(1,128)}), f32[4,1,32]{2,1,0:T(1,128)S(1)}, u32[]{:S(2)}, u32[]{:S(2)}) async-start(f32[4,1,32]{2,1,0:T(1,128)} %param.21), calls=%async_computation | async-start | bytes 4096 | tf_op jit(solution)/shard_map/all_to_all | solution.py:159
  6.7 5.2 %all-gather = f32[4,1,32]{2,1,0:T(1,128)S(1)} all-gather(f32[1,1,32]{2,1,0:T(1,128)S(1)} %bitcast.154), channel_id=1, replica_groups=mesh['tm'=4,'space'=8] {'tm'}, dimensions={0}, use_global_device_ids=true | all-gather | bytes 640 | tf_op jit(solution)/shard_map/all_gather | solution.py:157
  12.6 1.3 fusion.102
  13.9 8.2 %all_gather.10 = f32[4,4,32,256]{3,2,1,0:T(8,128)} all-gather(f32[1,4,32,256]{3,2,1,0:T(8,128)S(1)} %copy-done.7), channel_id=1, replica_groups=mesh['tm'=4,'space'=8] {'tm'}, dimensions={0}, use_global_device_ids=true | all-gather | bytes 655360 | tf_op jit(solution)/shard_map/all_gather | solution.py:156
  22.1 7.4 %all_gather.11 = f32[4,4,32,256]{3,2,1,0:T(8,128)S(1)} all-gather(f32[1,4,32,256]{3,2,1,0:T(8,128)S(1)} %copy-done.8), channel_id=1, replica_groups=mesh['tm'=4,'space'=8] {'tm'}, dimensions={0}, use_global_device_ids=true | all-gather | bytes 655360 | tf_op jit(solution)/shard_map/all_gather | solution.py:155
  29.6 5.2 %select_add_fusion = (f32[4,32,256]{2,1,0:T(8,128)S(1)}, pred[4,32,256]{2,1,0:T(8,128)(4,1)S(1)}, pred[4,32,256]{2,1,0:T(8,128)(4,1)S(1)}, pred[4,32,256]{2,1,0:...) fusion(f32[]{:T(128)} %bitcast.28, f32[]{:T(128)} %bitcast.27, ...), kind=kLoop, calls=%fused_computation.152 | loop fusion | flops 753664 | bytes 524320 | tf_op jit(solution)/shard_map/add | solution.py:96
  34.8 5.1 %add_multiply_fusion = f32[4,32,256]{2,1,0:T(8,128)S(1)} fusion(pred[4,32,256]{2,1,0:T(8,128)(4,1)S(1)} %get-tuple-element.474, pred[4,32,256]{2,1,0:T(8,128)(4,1)S(1)} %get-tuple-element.473, pred[4,32,256]{2,1,0:T(8,128)(4,1)S(1)} %get-tuple-element.472, pred[4,32,256]{2,1,0:T(8,128)(4,1)S(1)} %get-tuple-element.471, ...), kind=kLoop, calls=%fused_computation.153 | loop fusion | flops 524288 | bytes 393248 | tf_op jit(solution)/shard_map/mul | solution.py:100
  39.8 5.1 %select_add_fusion.1 = f32[4,32,256]{2,1,0:T(8,128)S(1)} fusion(pred[4,32,256]{2,1,0:T(8,128)(4,1)S(1)} %get-tuple-element.474, pred[4,32,256]{2,1,0:T(8,128)(4,1)S(1)} %get-tuple-element.473, pred[4,32,256]{2,1,0:T(8,128)(4,1)S(1)} %get-tuple-element.472, pred[4,32,256]{2,1,0:T(8,128)(4,1)S(1)} %get-tuple-element.471, ...), kind=kLoop, calls=%fused_computation.155 | loop fusion | flops 491520 | bytes 393248 | tf_op jit(solution)/shard_map/add | solution.py:96
  46.0 170.8 %while.24 = (s32[]{:T(128)}, f32[1,4,32,256]{3,2,1,0:T(8,128)S(1)}, f32[1,4,32,256]{3,2,1,0:T(8,128)S(1)}, f32[4,1,4,32,256]{4,3,2,1,0:T(8,128)}, f32[4,1,4,32,2...) while((s32[]{:T(128)}, f32[1,4,32,256]{3,2,1,0:T(8,128)S(1)}, ...), condition=%wide.region_3.4_spmd.clone, body=%wide.region_1.3_spmd.clone.sunk | while | flops 19529856 | bytes 16516069 | solution.py:182
  46.0 1.3 collective-permute-start
  47.3 4.5 %collective-permute-start.1 = (f32[2,1,1,32,256]{4,3,2,1,0:T(8,128)S(1)}, f32[2,1,1,32,256]{4,3,2,1,0:T(8,128)S(1)}, u32[]{:S(2)}, u32[]{:S(2)}) collective-permute-start(f32[2,1,1,32,256]{4,3,2,1,0:T(8,128)S(1)} %get-tuple-element.644), channel_id=1, source_target_pairs={{0,1},{1,2},{2,3},{3,4},{4,5},{5,6},{6,7},{8,9},{9,10},{10,11},{11... | collective-permute-start | bytes 196616 | tf_op jit(solution)/shard_map/while/body/eval_jaxpr/ppermute | solution.py:19
  52.4 1.6 collective-permute-done.1
  54.1 1.3 fusion.133
  55.4 1.3 collective-permute-start.2
  56.7 5.1 %collective-permute-start.3 = (f32[1,1,32,256]{3,2,1,0:T(8,128)S(1)}, f32[1,1,32,256]{3,2,1,0:T(8,128)S(1)}, u32[]{:S(2)}, u32[]{:S(2)}) collective-permute-start(f32[1,1,32,256]{3,2,1,0:T(8,128)S(1)} %get-tuple-element.656), channel_id=1, source_target_pairs={{0,1},{1,2},{2,3},{3,4},{4,5},{5,6},{6,7},{8,9},{9,10},{10,11},{11... | collective-permute-start | bytes 98312 | tf_op jit(solution)/shard_map/while/body/eval_jaxpr/ppermute | solution.py:19
  61.8 1.6 collective-permute-done.3
  63.6 1.3 collective-permute-start.4
  64.9 5.8 %collective-permute-start.5 = (f32[1,1,32,256]{3,2,1,0:T(8,128)S(1)}, f32[1,1,32,256]{3,2,1,0:T(8,128)S(1)}, u32[]{:S(2)}, u32[]{:S(2)}) collective-permute-start(f32[1,1,32,256]{3,2,1,0:T(8,128)S(1)} %get-tuple-element.658), channel_id=1, source_target_pairs={{0,1},{1,2},{2,3},{3,4},{4,5},{5,6},{6,7},{8,9},{9,10},{10,11},{11... | collective-permute-start | bytes 98312 | tf_op jit(solution)/shard_map/while/body/eval_jaxpr/ppermute | solution.py:19
  70.7 1.6 collective-permute-done.5
  72.9 1.6 constant_dynamic-update-slice_fusion.2
  74.4 1.4 collective-permute-start.6
  75.9 5.8 %collective-permute-start.7 = (f32[2,1,1,32,256]{4,3,2,1,0:T(8,128)S(1)}, f32[2,1,1,32,256]{4,3,2,1,0:T(8,128)S(1)}, u32[]{:S(2)}, u32[]{:S(2)}) collective-permute-start(f32[2,1,1,32,256]{4,3,2,1,0:T(8,128)S(1)} %get-tuple-element.662), channel_id=1, source_target_pairs={{0,1},{1,2},{2,3},{3,4},{4,5},{5,6},{6,7},{8,9},{9,10},{10,11},{11... | collective-permute-start | bytes 196616 | tf_op jit(solution)/shard_map/while/body/eval_jaxpr/ppermute | solution.py:19
  81.8 4.0 %fusion.137 = f32[]{:T(128)} fusion(f32[32]{0:T(128)S(1)} %get-tuple-element.718, f32[32768,1]{0,1:T(1,128)S(1)} %bitcast.144, s32[32768]{0:T(1024)S(1)} %copy-done.6, s32[32]{0:T(128)S(1)} %get-tuple-element.720, f32[1,4,32]{2,1,0:T(4,128)S(1)} %get-tuple-element.717, s32[]{:T(128)S(6)} %copy.28), kind=kOutput, calls=%fused_computation.10.clone.1 | convolution fusion | flops 14680191 | bytes 262536 | tf_op jit(solution)/shard_map/while/body/eval_jaxpr/dot_general | solution.py:148
  87.6 1.3 collective-permute-start
  88.9 5.8 %collective-permute-start.1 = (f32[2,1,1,32,256]{4,3,2,1,0:T(8,128)S(1)}, f32[2,1,1,32,256]{4,3,2,1,0:T(8,128)S(1)}, u32[]{:S(2)}, u32[]{:S(2)}) collective-permute-start(f32[2,1,1,32,256]{4,3,2,1,0:T(8,128)S(1)} %get-tuple-element.644), channel_id=1, source_target_pairs={{0,1},{1,2},{2,3},{3,4},{4,5},{5,6},{6,7},{8,9},{9,10},{10,11},{11... | collective-permute-start | bytes 196616 | tf_op jit(solution)/shard_map/while/body/eval_jaxpr/ppermute | solution.py:19
  95.0 1.6 collective-permute-done.1
  96.7 1.3 fusion.133
  98.0 1.3 collective-permute-start.2
  99.3 5.4 %collective-permute-start.3 = (f32[1,1,32,256]{3,2,1,0:T(8,128)S(1)}, f32[1,1,32,256]{3,2,1,0:T(8,128)S(1)}, u32[]{:S(2)}, u32[]{:S(2)}) collective-permute-start(f32[1,1,32,256]{3,2,1,0:T(8,128)S(1)} %get-tuple-element.656), channel_id=1, source_target_pairs={{0,1},{1,2},{2,3},{3,4},{4,5},{5,6},{6,7},{8,9},{9,10},{10,11},{11... | collective-permute-start | bytes 98312 | tf_op jit(solution)/shard_map/while/body/eval_jaxpr/ppermute | solution.py:19
  104.7 1.6 collective-permute-done.3
  106.5 1.3 collective-permute-start.4
  107.8 5.8 %collective-permute-start.5 = (f32[1,1,32,256]{3,2,1,0:T(8,128)S(1)}, f32[1,1,32,256]{3,2,1,0:T(8,128)S(1)}, u32[]{:S(2)}, u32[]{:S(2)}) collective-permute-start(f32[1,1,32,256]{3,2,1,0:T(8,128)S(1)} %get-tuple-element.658), channel_id=1, source_target_pairs={{0,1},{1,2},{2,3},{3,4},{4,5},{5,6},{6,7},{8,9},{9,10},{10,11},{11... | collective-permute-start | bytes 98312 | tf_op jit(solution)/shard_map/while/body/eval_jaxpr/ppermute | solution.py:19
  113.6 1.6 collective-permute-done.5
  115.8 1.6 constant_dynamic-update-slice_fusion.2
  117.4 1.4 collective-permute-start.6
  118.8 5.8 %collective-permute-start.7 = (f32[2,1,1,32,256]{4,3,2,1,0:T(8,128)S(1)}, f32[2,1,1,32,256]{4,3,2,1,0:T(8,128)S(1)}, u32[]{:S(2)}, u32[]{:S(2)}) collective-permute-start(f32[2,1,1,32,256]{4,3,2,1,0:T(8,128)S(1)} %get-tuple-element.662), channel_id=1, source_target_pairs={{0,1},{1,2},{2,3},{3,4},{4,5},{5,6},{6,7},{8,9},{9,10},{10,11},{11... | collective-permute-start | bytes 196616 | tf_op jit(solution)/shard_map/while/body/eval_jaxpr/ppermute | solution.py:19
  124.7 4.0 %fusion.137 = f32[]{:T(128)} fusion(f32[32]{0:T(128)S(1)} %get-tuple-element.718, f32[32768,1]{0,1:T(1,128)S(1)} %bitcast.144, s32[32768]{0:T(1024)S(1)} %copy-done.6, s32[32]{0:T(128)S(1)} %get-tuple-element.720, f32[1,4,32]{2,1,0:T(4,128)S(1)} %get-tuple-element.717, s32[]{:T(128)S(6)} %copy.28), kind=kOutput, calls=%fused_computation.10.clone.1 | convolution fusion | flops 14680191 | bytes 262536 | tf_op jit(solution)/shard_map/while/body/eval_jaxpr/dot_general | solution.py:148
  130.5 1.3 collective-permute-start
  131.8 5.9 %collective-permute-start.1 = (f32[2,1,1,32,256]{4,3,2,1,0:T(8,128)S(1)}, f32[2,1,1,32,256]{4,3,2,1,0:T(8,128)S(1)}, u32[]{:S(2)}, u32[]{:S(2)}) collective-permute-start(f32[2,1,1,32,256]{4,3,2,1,0:T(8,128)S(1)} %get-tuple-element.644), channel_id=1, source_target_pairs={{0,1},{1,2},{2,3},{3,4},{4,5},{5,6},{6,7},{8,9},{9,10},{10,11},{11... | collective-permute-start | bytes 196616 | tf_op jit(solution)/shard_map/while/body/eval_jaxpr/ppermute | solution.py:19
  138.1 1.7 collective-permute-done.1
  139.9 1.3 fusion.133
  142.6 5.4 %collective-permute-start.3 = (f32[1,1,32,256]{3,2,1,0:T(8,128)S(1)}, f32[1,1,32,256]{3,2,1,0:T(8,128)S(1)}, u32[]{:S(2)}, u32[]{:S(2)}) collective-permute-start(f32[1,1,32,256]{3,2,1,0:T(8,128)S(1)} %get-tuple-element.656), channel_id=1, source_target_pairs={{0,1},{1,2},{2,3},{3,4},{4,5},{5,6},{6,7},{8,9},{9,10},{10,11},{11... | collective-permute-start | bytes 98312 | tf_op jit(solution)/shard_map/while/body/eval_jaxpr/ppermute | solution.py:19
  148.0 1.6 collective-permute-done.3
  149.7 1.3 collective-permute-start.4
  151.0 5.9 %collective-permute-start.5 = (f32[1,1,32,256]{3,2,1,0:T(8,128)S(1)}, f32[1,1,32,256]{3,2,1,0:T(8,128)S(1)}, u32[]{:S(2)}, u32[]{:S(2)}) collective-permute-start(f32[1,1,32,256]{3,2,1,0:T(8,128)S(1)} %get-tuple-element.658), channel_id=1, source_target_pairs={{0,1},{1,2},{2,3},{3,4},{4,5},{5,6},{6,7},{8,9},{9,10},{10,11},{11... | collective-permute-start | bytes 98312 | tf_op jit(solution)/shard_map/while/body/eval_jaxpr/ppermute | solution.py:19
  157.1 1.5 collective-permute-done.5
  159.2 1.6 constant_dynamic-update-slice_fusion.2
  160.8 1.4 collective-permute-start.6
  162.2 5.7 %collective-permute-start.7 = (f32[2,1,1,32,256]{4,3,2,1,0:T(8,128)S(1)}, f32[2,1,1,32,256]{4,3,2,1,0:T(8,128)S(1)}, u32[]{:S(2)}, u32[]{:S(2)}) collective-permute-start(f32[2,1,1,32,256]{4,3,2,1,0:T(8,128)S(1)} %get-tuple-element.662), channel_id=1, source_target_pairs={{0,1},{1,2},{2,3},{3,4},{4,5},{5,6},{6,7},{8,9},{9,10},{10,11},{11... | collective-permute-start | bytes 196616 | tf_op jit(solution)/shard_map/while/body/eval_jaxpr/ppermute | solution.py:19
  168.1 4.0 %fusion.137 = f32[]{:T(128)} fusion(f32[32]{0:T(128)S(1)} %get-tuple-element.718, f32[32768,1]{0,1:T(1,128)S(1)} %bitcast.144, s32[32768]{0:T(1024)S(1)} %copy-done.6, s32[32]{0:T(128)S(1)} %get-tuple-element.720, f32[1,4,32]{2,1,0:T(4,128)S(1)} %get-tuple-element.717, s32[]{:T(128)S(6)} %copy.28), kind=kOutput, calls=%fused_computation.10.clone.1 | convolution fusion | flops 14680191 | bytes 262536 | tf_op jit(solution)/shard_map/while/body/eval_jaxpr/dot_general | solution.py:148
  175.2 5.8 %collective-permute-start.1 = (f32[2,1,1,32,256]{4,3,2,1,0:T(8,128)S(1)}, f32[2,1,1,32,256]{4,3,2,1,0:T(8,128)S(1)}, u32[]{:S(2)}, u32[]{:S(2)}) collective-permute-start(f32[2,1,1,32,256]{4,3,2,1,0:T(8,128)S(1)} %get-tuple-element.644), channel_id=1, source_target_pairs={{0,1},{1,2},{2,3},{3,4},{4,5},{5,6},{6,7},{8,9},{9,10},{10,11},{11... | collective-permute-start | bytes 196616 | tf_op jit(solution)/shard_map/while/body/eval_jaxpr/ppermute | solution.py:19
  181.3 1.6 collective-permute-done.1
  183.0 1.3 fusion.133
  185.6 5.4 %collective-permute-start.3 = (f32[1,1,32,256]{3,2,1,0:T(8,128)S(1)}, f32[1,1,32,256]{3,2,1,0:T(8,128)S(1)}, u32[]{:S(2)}, u32[]{:S(2)}) collective-permute-start(f32[1,1,32,256]{3,2,1,0:T(8,128)S(1)} %get-tuple-element.656), channel_id=1, source_target_pairs={{0,1},{1,2},{2,3},{3,4},{4,5},{5,6},{6,7},{8,9},{9,10},{10,11},{11... | collective-permute-start | bytes 98312 | tf_op jit(solution)/shard_map/while/body/eval_jaxpr/ppermute | solution.py:19
  191.0 1.6 collective-permute-done.3
  194.1 5.8 %collective-permute-start.5 = (f32[1,1,32,256]{3,2,1,0:T(8,128)S(1)}, f32[1,1,32,256]{3,2,1,0:T(8,128)S(1)}, u32[]{:S(2)}, u32[]{:S(2)}) collective-permute-start(f32[1,1,32,256]{3,2,1,0:T(8,128)S(1)} %get-tuple-element.658), channel_id=1, source_target_pairs={{0,1},{1,2},{2,3},{3,4},{4,5},{5,6},{6,7},{8,9},{9,10},{10,11},{11... | collective-permute-start | bytes 98312 | tf_op jit(solution)/shard_map/while/body/eval_jaxpr/ppermute | solution.py:19
  199.9 1.6 collective-permute-done.5
  202.1 1.6 constant_dynamic-update-slice_fusion.2
  203.7 1.4 collective-permute-start.6
  205.1 5.8 %collective-permute-start.7 = (f32[2,1,1,32,256]{4,3,2,1,0:T(8,128)S(1)}, f32[2,1,1,32,256]{4,3,2,1,0:T(8,128)S(1)}, u32[]{:S(2)}, u32[]{:S(2)}) collective-permute-start(f32[2,1,1,32,256]{4,3,2,1,0:T(8,128)S(1)} %get-tuple-element.662), channel_id=1, source_target_pairs={{0,1},{1,2},{2,3},{3,4},{4,5},{5,6},{6,7},{8,9},{9,10},{10,11},{11... | collective-permute-start | bytes 196616 | tf_op jit(solution)/shard_map/while/body/eval_jaxpr/ppermute | solution.py:19
  211.0 4.0 %fusion.137 = f32[]{:T(128)} fusion(f32[32]{0:T(128)S(1)} %get-tuple-element.718, f32[32768,1]{0,1:T(1,128)S(1)} %bitcast.144, s32[32768]{0:T(1024)S(1)} %copy-done.6, s32[32]{0:T(128)S(1)} %get-tuple-element.720, f32[1,4,32]{2,1,0:T(4,128)S(1)} %get-tuple-element.717, s32[]{:T(128)S(6)} %copy.28), kind=kOutput, calls=%fused_computation.10.clone.1 | convolution fusion | flops 14680191 | bytes 262536 | tf_op jit(solution)/shard_map/while/body/eval_jaxpr/dot_general | solution.py:148
  216.8 12.3 %all_to_all.36 = f32[4,1,4,32,256]{4,3,2,1,0:T(8,128)S(1)} all-to-all(f32[4,1,4,32,256]{4,3,2,1,0:T(8,128)} %get-tuple-element.380), channel_id=1, replica_groups=mesh['tm'=4,'space'=8] {'tm'}, dimensions={0} | all-to-all | bytes 1048576 | tf_op jit(solution)/shard_map/all_to_all | solution.py:189
  229.0 3.5 %all-to-all-start.2 = ((f32[4,1,4,32,256]{4,3,2,1,0:T(8,128)}), f32[4,1,4,32,256]{4,3,2,1,0:T(8,128)S(1)}, u32[]{:S(2)}, u32[]{:S(2)}) async-start(f32[4,1,4,32,256]{4,3,2,1,0:T(8,128)} %get-tuple-element.381), calls=%async_computation.2 | async-start | bytes 1048576 | tf_op jit(solution)/shard_map/all_to_all | solution.py:190
  232.6 46.4 %psum.7 = f32[4]{0:T(128)S(1)} all-reduce(f32[4]{0:T(128)S(1)} %dynamic_update_slice.24), channel_id=1, replica_groups=mesh['tm'=4,'space'=8] {'tm','space'}, use_global_device_ids=true, to_apply=%region_4.5 | all-reduce | flops 4 | bytes 32 | tf_op jit(solution)/shard_map/psum | solution.py:193
  (149 shorter events, 20.7 us)
Async XLA Ops:
  0.6 28.9 %copy-start = (f32[4,4,32,256]{3,2,1,0:T(8,128)S(1)}, f32[4,4,32,256]{3,2,1,0:T(8,128)}, u32[]{:S(2)}) copy-start(f32[4,4,32,256]{3,2,1,0:T(8,128)} %param.12) | copy-start | bytes 1572868
  0.6 4.4 %copy-start.10 = (f32[3,8]{1,0:T(4,128)S(1)}, f32[3,8]{1,0:T(4,128)}, u32[]{:S(2)}) copy-start(f32[3,8]{1,0:T(4,128)} %param.18) | copy-start | bytes 292
  0.7 11.2 %copy-start.11 = (s32[32]{0:T(128)S(1)}, s32[32]{0:T(128)}, u32[]{:S(2)}) copy-start(s32[32]{0:T(128)} %param.19) | copy-start | bytes 388
  0.7 6.0 %copy-start.12 = (f32[1,32]{1,0:T(1,128)S(1)}, f32[1,32]{1,0:T(1,128)}, u32[]{:S(2)}) copy-start(f32[1,32]{1,0:T(1,128)} %param.20) | copy-start | bytes 388
  0.7 44.4 %all-to-all-start = ((f32[4,1,32]{2,1,0:T(1,128)}), f32[4,1,32]{2,1,0:T(1,128)S(1)}, u32[]{:S(2)}, u32[]{:S(2)}) async-start(f32[4,1,32]{2,1,0:T(1,128)} %param.21), calls=%async_computation | async-start | bytes 4096 | tf_op jit(solution)/shard_map/all_to_all | solution.py:159
  6.6 7.3 %copy-start.5 = (s32[16,2,8,128]{3,1,2,0:T(2,128)}, s32[16,2,8,128]{3,1,2,0:T(2,128)S(1)}, u32[]{:S(2)}) copy-start(s32[16,2,8,128]{3,1,2,0:T(2,128)S(1)} %copy.16) | copy-start | bytes 393220
  12.6 1.4 copy-start.7
  13.9 8.2 %copy-start.8 = (f32[1,4,32,256]{3,2,1,0:T(8,128)S(1)}, f32[1,4,32,256]{3,2,1,0:T(8,128)}, u32[]{:S(2)}) copy-start(f32[1,4,32,256]{3,2,1,0:T(8,128)} %param.13) | copy-start | bytes 393220
  22.1 7.4 %copy-start.9 = (s32[4,32,256]{2,1,0:T(8,128)S(1)}, s32[4,32,256]{2,1,0:T(8,128)}, u32[]{:S(2)}) copy-start(s32[4,32,256]{2,1,0:T(8,128)} %param.17) | copy-start | bytes 393220
  45.0 0.9 copy-start.1
  45.0 1.0 copy-start.2
  46.0 6.4 %collective-permute-start = (f32[2,1,1,32,256]{4,3,2,1,0:T(8,128)S(1)}, f32[2,1,1,32,256]{4,3,2,1,0:T(8,128)S(1)}, u32[]{:S(2)}, u32[]{:S(2)}) collective-permute-start(f32[2,1,1,32,256]{4,3,2,1,0:T(8,128)S(1)} %get-tuple-element.643), channel_id=1, source_target_pairs={{1,0},{2,1},{3,2},{4,3},{5,4},{6,5},{7,6},{9,8},{10,9},{11,10},{12... | collective-permute-start | bytes 196616 | tf_op jit(solution)/shard_map/while/body/eval_jaxpr/ppermute | solution.py:21
  47.3 6.7 %collective-permute-start.1 = (f32[2,1,1,32,256]{4,3,2,1,0:T(8,128)S(1)}, f32[2,1,1,32,256]{4,3,2,1,0:T(8,128)S(1)}, u32[]{:S(2)}, u32[]{:S(2)}) collective-permute-start(f32[2,1,1,32,256]{4,3,2,1,0:T(8,128)S(1)} %get-tuple-element.644), channel_id=1, source_target_pairs={{0,1},{1,2},{2,3},{3,4},{4,5},{5,6},{6,7},{8,9},{9,10},{10,11},{11... | collective-permute-start | bytes 196616 | tf_op jit(solution)/shard_map/while/body/eval_jaxpr/ppermute | solution.py:19
  55.4 6.4 %collective-permute-start.2 = (f32[1,1,32,256]{3,2,1,0:T(8,128)S(1)}, f32[1,1,32,256]{3,2,1,0:T(8,128)S(1)}, u32[]{:S(2)}, u32[]{:S(2)}) collective-permute-start(f32[1,1,32,256]{3,2,1,0:T(8,128)S(1)} %get-tuple-element.655), channel_id=1, source_target_pairs={{1,0},{2,1},{3,2},{4,3},{5,4},{6,5},{7,6},{9,8},{10,9},{11,10},{12... | collective-permute-start | bytes 98312 | tf_op jit(solution)/shard_map/while/body/eval_jaxpr/ppermute | solution.py:21
  56.7 6.7 %collective-permute-start.3 = (f32[1,1,32,256]{3,2,1,0:T(8,128)S(1)}, f32[1,1,32,256]{3,2,1,0:T(8,128)S(1)}, u32[]{:S(2)}, u32[]{:S(2)}) collective-permute-start(f32[1,1,32,256]{3,2,1,0:T(8,128)S(1)} %get-tuple-element.656), channel_id=1, source_target_pairs={{0,1},{1,2},{2,3},{3,4},{4,5},{5,6},{6,7},{8,9},{9,10},{10,11},{11... | collective-permute-start | bytes 98312 | tf_op jit(solution)/shard_map/while/body/eval_jaxpr/ppermute | solution.py:19
  63.6 7.1 %collective-permute-start.4 = (f32[1,1,32,256]{3,2,1,0:T(8,128)S(1)}, f32[1,1,32,256]{3,2,1,0:T(8,128)S(1)}, u32[]{:S(2)}, u32[]{:S(2)}) collective-permute-start(f32[1,1,32,256]{3,2,1,0:T(8,128)S(1)} %get-tuple-element.657), channel_id=1, source_target_pairs={{1,0},{2,1},{3,2},{4,3},{5,4},{6,5},{7,6},{9,8},{10,9},{11,10},{12... | collective-permute-start | bytes 98312 | tf_op jit(solution)/shard_map/while/body/eval_jaxpr/ppermute | solution.py:21
  64.9 7.4 %collective-permute-start.5 = (f32[1,1,32,256]{3,2,1,0:T(8,128)S(1)}, f32[1,1,32,256]{3,2,1,0:T(8,128)S(1)}, u32[]{:S(2)}, u32[]{:S(2)}) collective-permute-start(f32[1,1,32,256]{3,2,1,0:T(8,128)S(1)} %get-tuple-element.658), channel_id=1, source_target_pairs={{0,1},{1,2},{2,3},{3,4},{4,5},{5,6},{6,7},{8,9},{9,10},{10,11},{11... | collective-permute-start | bytes 98312 | tf_op jit(solution)/shard_map/while/body/eval_jaxpr/ppermute | solution.py:19
  70.7 1.6 copy-start.3
  72.3 0.6 copy-start.4
  74.4 7.4 %copy-start.6 = (s32[32768]{0:T(1024)S(1)}, s32[32768]{0:T(1024)}, u32[]{:S(2)}) copy-start(s32[32768]{0:T(1024)} %get-tuple-element.719) | copy-start | bytes 393220 | tf_op jit(solution)/shard_map/while
  74.4 12.0 %collective-permute-start.6 = (f32[2,1,1,32,256]{4,3,2,1,0:T(8,128)S(1)}, f32[2,1,1,32,256]{4,3,2,1,0:T(8,128)S(1)}, u32[]{:S(2)}, u32[]{:S(2)}) collective-permute-start(f32[2,1,1,32,256]{4,3,2,1,0:T(8,128)S(1)} %get-tuple-element.661), channel_id=1, source_target_pairs={{1,0},{2,1},{3,2},{4,3},{5,4},{6,5},{7,6},{9,8},{10,9},{11,10},{12... | collective-permute-start | bytes 196616 | tf_op jit(solution)/shard_map/while/body/eval_jaxpr/ppermute | solution.py:21
  75.9 10.6 %collective-permute-start.7 = (f32[2,1,1,32,256]{4,3,2,1,0:T(8,128)S(1)}, f32[2,1,1,32,256]{4,3,2,1,0:T(8,128)S(1)}, u32[]{:S(2)}, u32[]{:S(2)}) collective-permute-start(f32[2,1,1,32,256]{4,3,2,1,0:T(8,128)S(1)} %get-tuple-element.662), channel_id=1, source_target_pairs={{0,1},{1,2},{2,3},{3,4},{4,5},{5,6},{6,7},{8,9},{9,10},{10,11},{11... | collective-permute-start | bytes 196616 | tf_op jit(solution)/shard_map/while/body/eval_jaxpr/ppermute | solution.py:19
  87.6 7.4 %collective-permute-start = (f32[2,1,1,32,256]{4,3,2,1,0:T(8,128)S(1)}, f32[2,1,1,32,256]{4,3,2,1,0:T(8,128)S(1)}, u32[]{:S(2)}, u32[]{:S(2)}) collective-permute-start(f32[2,1,1,32,256]{4,3,2,1,0:T(8,128)S(1)} %get-tuple-element.643), channel_id=1, source_target_pairs={{1,0},{2,1},{3,2},{4,3},{5,4},{6,5},{7,6},{9,8},{10,9},{11,10},{12... | collective-permute-start | bytes 196616 | tf_op jit(solution)/shard_map/while/body/eval_jaxpr/ppermute | solution.py:21
  88.9 7.6 %collective-permute-start.1 = (f32[2,1,1,32,256]{4,3,2,1,0:T(8,128)S(1)}, f32[2,1,1,32,256]{4,3,2,1,0:T(8,128)S(1)}, u32[]{:S(2)}, u32[]{:S(2)}) collective-permute-start(f32[2,1,1,32,256]{4,3,2,1,0:T(8,128)S(1)} %get-tuple-element.644), channel_id=1, source_target_pairs={{0,1},{1,2},{2,3},{3,4},{4,5},{5,6},{6,7},{8,9},{9,10},{10,11},{11... | collective-permute-start | bytes 196616 | tf_op jit(solution)/shard_map/while/body/eval_jaxpr/ppermute | solution.py:19
  98.0 6.8 %collective-permute-start.2 = (f32[1,1,32,256]{3,2,1,0:T(8,128)S(1)}, f32[1,1,32,256]{3,2,1,0:T(8,128)S(1)}, u32[]{:S(2)}, u32[]{:S(2)}) collective-permute-start(f32[1,1,32,256]{3,2,1,0:T(8,128)S(1)} %get-tuple-element.655), channel_id=1, source_target_pairs={{1,0},{2,1},{3,2},{4,3},{5,4},{6,5},{7,6},{9,8},{10,9},{11,10},{12... | collective-permute-start | bytes 98312 | tf_op jit(solution)/shard_map/while/body/eval_jaxpr/ppermute | solution.py:21
  99.3 7.0 %collective-permute-start.3 = (f32[1,1,32,256]{3,2,1,0:T(8,128)S(1)}, f32[1,1,32,256]{3,2,1,0:T(8,128)S(1)}, u32[]{:S(2)}, u32[]{:S(2)}) collective-permute-start(f32[1,1,32,256]{3,2,1,0:T(8,128)S(1)} %get-tuple-element.656), channel_id=1, source_target_pairs={{0,1},{1,2},{2,3},{3,4},{4,5},{5,6},{6,7},{8,9},{9,10},{10,11},{11... | collective-permute-start | bytes 98312 | tf_op jit(solution)/shard_map/while/body/eval_jaxpr/ppermute | solution.py:19
  106.5 7.1 %collective-permute-start.4 = (f32[1,1,32,256]{3,2,1,0:T(8,128)S(1)}, f32[1,1,32,256]{3,2,1,0:T(8,128)S(1)}, u32[]{:S(2)}, u32[]{:S(2)}) collective-permute-start(f32[1,1,32,256]{3,2,1,0:T(8,128)S(1)} %get-tuple-element.657), channel_id=1, source_target_pairs={{1,0},{2,1},{3,2},{4,3},{5,4},{6,5},{7,6},{9,8},{10,9},{11,10},{12... | collective-permute-start | bytes 98312 | tf_op jit(solution)/shard_map/while/body/eval_jaxpr/ppermute | solution.py:21
  107.8 7.4 %collective-permute-start.5 = (f32[1,1,32,256]{3,2,1,0:T(8,128)S(1)}, f32[1,1,32,256]{3,2,1,0:T(8,128)S(1)}, u32[]{:S(2)}, u32[]{:S(2)}) collective-permute-start(f32[1,1,32,256]{3,2,1,0:T(8,128)S(1)} %get-tuple-element.658), channel_id=1, source_target_pairs={{0,1},{1,2},{2,3},{3,4},{4,5},{5,6},{6,7},{8,9},{9,10},{10,11},{11... | collective-permute-start | bytes 98312 | tf_op jit(solution)/shard_map/while/body/eval_jaxpr/ppermute | solution.py:19
  113.6 1.6 copy-start.3
  115.2 0.6 copy-start.4
  117.3 7.4 %copy-start.6 = (s32[32768]{0:T(1024)S(1)}, s32[32768]{0:T(1024)}, u32[]{:S(2)}) copy-start(s32[32768]{0:T(1024)} %get-tuple-element.719) | copy-start | bytes 393220 | tf_op jit(solution)/shard_map/while
  117.4 12.0 %collective-permute-start.6 = (f32[2,1,1,32,256]{4,3,2,1,0:T(8,128)S(1)}, f32[2,1,1,32,256]{4,3,2,1,0:T(8,128)S(1)}, u32[]{:S(2)}, u32[]{:S(2)}) collective-permute-start(f32[2,1,1,32,256]{4,3,2,1,0:T(8,128)S(1)} %get-tuple-element.661), channel_id=1, source_target_pairs={{1,0},{2,1},{3,2},{4,3},{5,4},{6,5},{7,6},{9,8},{10,9},{11,10},{12... | collective-permute-start | bytes 196616 | tf_op jit(solution)/shard_map/while/body/eval_jaxpr/ppermute | solution.py:21
  118.8 10.6 %collective-permute-start.7 = (f32[2,1,1,32,256]{4,3,2,1,0:T(8,128)S(1)}, f32[2,1,1,32,256]{4,3,2,1,0:T(8,128)S(1)}, u32[]{:S(2)}, u32[]{:S(2)}) collective-permute-start(f32[2,1,1,32,256]{4,3,2,1,0:T(8,128)S(1)} %get-tuple-element.662), channel_id=1, source_target_pairs={{0,1},{1,2},{2,3},{3,4},{4,5},{5,6},{6,7},{8,9},{9,10},{10,11},{11... | collective-permute-start | bytes 196616 | tf_op jit(solution)/shard_map/while/body/eval_jaxpr/ppermute | solution.py:19
  130.5 7.6 %collective-permute-start = (f32[2,1,1,32,256]{4,3,2,1,0:T(8,128)S(1)}, f32[2,1,1,32,256]{4,3,2,1,0:T(8,128)S(1)}, u32[]{:S(2)}, u32[]{:S(2)}) collective-permute-start(f32[2,1,1,32,256]{4,3,2,1,0:T(8,128)S(1)} %get-tuple-element.643), channel_id=1, source_target_pairs={{1,0},{2,1},{3,2},{4,3},{5,4},{6,5},{7,6},{9,8},{10,9},{11,10},{12... | collective-permute-start | bytes 196616 | tf_op jit(solution)/shard_map/while/body/eval_jaxpr/ppermute | solution.py:21
  131.8 8.0 %collective-permute-start.1 = (f32[2,1,1,32,256]{4,3,2,1,0:T(8,128)S(1)}, f32[2,1,1,32,256]{4,3,2,1,0:T(8,128)S(1)}, u32[]{:S(2)}, u32[]{:S(2)}) collective-permute-start(f32[2,1,1,32,256]{4,3,2,1,0:T(8,128)S(1)} %get-tuple-element.644), channel_id=1, source_target_pairs={{0,1},{1,2},{2,3},{3,4},{4,5},{5,6},{6,7},{8,9},{9,10},{10,11},{11... | collective-permute-start | bytes 196616 | tf_op jit(solution)/shard_map/while/body/eval_jaxpr/ppermute | solution.py:19
  141.3 6.7 %collective-permute-start.2 = (f32[1,1,32,256]{3,2,1,0:T(8,128)S(1)}, f32[1,1,32,256]{3,2,1,0:T(8,128)S(1)}, u32[]{:S(2)}, u32[]{:S(2)}) collective-permute-start(f32[1,1,32,256]{3,2,1,0:T(8,128)S(1)} %get-tuple-element.655), channel_id=1, source_target_pairs={{1,0},{2,1},{3,2},{4,3},{5,4},{6,5},{7,6},{9,8},{10,9},{11,10},{12... | collective-permute-start | bytes 98312 | tf_op jit(solution)/shard_map/while/body/eval_jaxpr/ppermute | solution.py:21
  142.6 7.0 %collective-permute-start.3 = (f32[1,1,32,256]{3,2,1,0:T(8,128)S(1)}, f32[1,1,32,256]{3,2,1,0:T(8,128)S(1)}, u32[]{:S(2)}, u32[]{:S(2)}) collective-permute-start(f32[1,1,32,256]{3,2,1,0:T(8,128)S(1)} %get-tuple-element.656), channel_id=1, source_target_pairs={{0,1},{1,2},{2,3},{3,4},{4,5},{5,6},{6,7},{8,9},{9,10},{10,11},{11... | collective-permute-start | bytes 98312 | tf_op jit(solution)/shard_map/while/body/eval_jaxpr/ppermute | solution.py:19
  149.7 7.3 %collective-permute-start.4 = (f32[1,1,32,256]{3,2,1,0:T(8,128)S(1)}, f32[1,1,32,256]{3,2,1,0:T(8,128)S(1)}, u32[]{:S(2)}, u32[]{:S(2)}) collective-permute-start(f32[1,1,32,256]{3,2,1,0:T(8,128)S(1)} %get-tuple-element.657), channel_id=1, source_target_pairs={{1,0},{2,1},{3,2},{4,3},{5,4},{6,5},{7,6},{9,8},{10,9},{11,10},{12... | collective-permute-start | bytes 98312 | tf_op jit(solution)/shard_map/while/body/eval_jaxpr/ppermute | solution.py:21
  151.0 7.6 %collective-permute-start.5 = (f32[1,1,32,256]{3,2,1,0:T(8,128)S(1)}, f32[1,1,32,256]{3,2,1,0:T(8,128)S(1)}, u32[]{:S(2)}, u32[]{:S(2)}) collective-permute-start(f32[1,1,32,256]{3,2,1,0:T(8,128)S(1)} %get-tuple-element.658), channel_id=1, source_target_pairs={{0,1},{1,2},{2,3},{3,4},{4,5},{5,6},{6,7},{8,9},{9,10},{10,11},{11... | collective-permute-start | bytes 98312 | tf_op jit(solution)/shard_map/while/body/eval_jaxpr/ppermute | solution.py:19
  157.1 1.5 copy-start.3
  158.6 0.6 copy-start.4
  160.8 7.3 %copy-start.6 = (s32[32768]{0:T(1024)S(1)}, s32[32768]{0:T(1024)}, u32[]{:S(2)}) copy-start(s32[32768]{0:T(1024)} %get-tuple-element.719) | copy-start | bytes 393220 | tf_op jit(solution)/shard_map/while
  160.8 12.0 %collective-permute-start.6 = (f32[2,1,1,32,256]{4,3,2,1,0:T(8,128)S(1)}, f32[2,1,1,32,256]{4,3,2,1,0:T(8,128)S(1)}, u32[]{:S(2)}, u32[]{:S(2)}) collective-permute-start(f32[2,1,1,32,256]{4,3,2,1,0:T(8,128)S(1)} %get-tuple-element.661), channel_id=1, source_target_pairs={{1,0},{2,1},{3,2},{4,3},{5,4},{6,5},{7,6},{9,8},{10,9},{11,10},{12... | collective-permute-start | bytes 196616 | tf_op jit(solution)/shard_map/while/body/eval_jaxpr/ppermute | solution.py:21
  162.2 10.5 %collective-permute-start.7 = (f32[2,1,1,32,256]{4,3,2,1,0:T(8,128)S(1)}, f32[2,1,1,32,256]{4,3,2,1,0:T(8,128)S(1)}, u32[]{:S(2)}, u32[]{:S(2)}) collective-permute-start(f32[2,1,1,32,256]{4,3,2,1,0:T(8,128)S(1)} %get-tuple-element.662), channel_id=1, source_target_pairs={{0,1},{1,2},{2,3},{3,4},{4,5},{5,6},{6,7},{8,9},{9,10},{10,11},{11... | collective-permute-start | bytes 196616 | tf_op jit(solution)/shard_map/while/body/eval_jaxpr/ppermute | solution.py:19
  173.9 7.4 %collective-permute-start = (f32[2,1,1,32,256]{4,3,2,1,0:T(8,128)S(1)}, f32[2,1,1,32,256]{4,3,2,1,0:T(8,128)S(1)}, u32[]{:S(2)}, u32[]{:S(2)}) collective-permute-start(f32[2,1,1,32,256]{4,3,2,1,0:T(8,128)S(1)} %get-tuple-element.643), channel_id=1, source_target_pairs={{1,0},{2,1},{3,2},{4,3},{5,4},{6,5},{7,6},{9,8},{10,9},{11,10},{12... | collective-permute-start | bytes 196616 | tf_op jit(solution)/shard_map/while/body/eval_jaxpr/ppermute | solution.py:21
  175.2 7.6 %collective-permute-start.1 = (f32[2,1,1,32,256]{4,3,2,1,0:T(8,128)S(1)}, f32[2,1,1,32,256]{4,3,2,1,0:T(8,128)S(1)}, u32[]{:S(2)}, u32[]{:S(2)}) collective-permute-start(f32[2,1,1,32,256]{4,3,2,1,0:T(8,128)S(1)} %get-tuple-element.644), channel_id=1, source_target_pairs={{0,1},{1,2},{2,3},{3,4},{4,5},{5,6},{6,7},{8,9},{9,10},{10,11},{11... | collective-permute-start | bytes 196616 | tf_op jit(solution)/shard_map/while/body/eval_jaxpr/ppermute | solution.py:19
  184.3 6.8 %collective-permute-start.2 = (f32[1,1,32,256]{3,2,1,0:T(8,128)S(1)}, f32[1,1,32,256]{3,2,1,0:T(8,128)S(1)}, u32[]{:S(2)}, u32[]{:S(2)}) collective-permute-start(f32[1,1,32,256]{3,2,1,0:T(8,128)S(1)} %get-tuple-element.655), channel_id=1, source_target_pairs={{1,0},{2,1},{3,2},{4,3},{5,4},{6,5},{7,6},{9,8},{10,9},{11,10},{12... | collective-permute-start | bytes 98312 | tf_op jit(solution)/shard_map/while/body/eval_jaxpr/ppermute | solution.py:21
  185.6 7.0 %collective-permute-start.3 = (f32[1,1,32,256]{3,2,1,0:T(8,128)S(1)}, f32[1,1,32,256]{3,2,1,0:T(8,128)S(1)}, u32[]{:S(2)}, u32[]{:S(2)}) collective-permute-start(f32[1,1,32,256]{3,2,1,0:T(8,128)S(1)} %get-tuple-element.656), channel_id=1, source_target_pairs={{0,1},{1,2},{2,3},{3,4},{4,5},{5,6},{6,7},{8,9},{9,10},{10,11},{11... | collective-permute-start | bytes 98312 | tf_op jit(solution)/shard_map/while/body/eval_jaxpr/ppermute | solution.py:19
  192.8 7.1 %collective-permute-start.4 = (f32[1,1,32,256]{3,2,1,0:T(8,128)S(1)}, f32[1,1,32,256]{3,2,1,0:T(8,128)S(1)}, u32[]{:S(2)}, u32[]{:S(2)}) collective-permute-start(f32[1,1,32,256]{3,2,1,0:T(8,128)S(1)} %get-tuple-element.657), channel_id=1, source_target_pairs={{1,0},{2,1},{3,2},{4,3},{5,4},{6,5},{7,6},{9,8},{10,9},{11,10},{12... | collective-permute-start | bytes 98312 | tf_op jit(solution)/shard_map/while/body/eval_jaxpr/ppermute | solution.py:21
  194.1 7.4 %collective-permute-start.5 = (f32[1,1,32,256]{3,2,1,0:T(8,128)S(1)}, f32[1,1,32,256]{3,2,1,0:T(8,128)S(1)}, u32[]{:S(2)}, u32[]{:S(2)}) collective-permute-start(f32[1,1,32,256]{3,2,1,0:T(8,128)S(1)} %get-tuple-element.658), channel_id=1, source_target_pairs={{0,1},{1,2},{2,3},{3,4},{4,5},{5,6},{6,7},{8,9},{9,10},{10,11},{11... | collective-permute-start | bytes 98312 | tf_op jit(solution)/shard_map/while/body/eval_jaxpr/ppermute | solution.py:19
  199.9 1.6 copy-start.3
  201.5 0.6 copy-start.4
  203.6 7.4 %copy-start.6 = (s32[32768]{0:T(1024)S(1)}, s32[32768]{0:T(1024)}, u32[]{:S(2)}) copy-start(s32[32768]{0:T(1024)} %get-tuple-element.719) | copy-start | bytes 393220 | tf_op jit(solution)/shard_map/while
  203.7 12.0 %collective-permute-start.6 = (f32[2,1,1,32,256]{4,3,2,1,0:T(8,128)S(1)}, f32[2,1,1,32,256]{4,3,2,1,0:T(8,128)S(1)}, u32[]{:S(2)}, u32[]{:S(2)}) collective-permute-start(f32[2,1,1,32,256]{4,3,2,1,0:T(8,128)S(1)} %get-tuple-element.661), channel_id=1, source_target_pairs={{1,0},{2,1},{3,2},{4,3},{5,4},{6,5},{7,6},{9,8},{10,9},{11,10},{12... | collective-permute-start | bytes 196616 | tf_op jit(solution)/shard_map/while/body/eval_jaxpr/ppermute | solution.py:21
  205.1 10.6 %collective-permute-start.7 = (f32[2,1,1,32,256]{4,3,2,1,0:T(8,128)S(1)}, f32[2,1,1,32,256]{4,3,2,1,0:T(8,128)S(1)}, u32[]{:S(2)}, u32[]{:S(2)}) collective-permute-start(f32[2,1,1,32,256]{4,3,2,1,0:T(8,128)S(1)} %get-tuple-element.662), channel_id=1, source_target_pairs={{0,1},{1,2},{2,3},{3,4},{4,5},{5,6},{6,7},{8,9},{9,10},{10,11},{11... | collective-permute-start | bytes 196616 | tf_op jit(solution)/shard_map/while/body/eval_jaxpr/ppermute | solution.py:19
  229.0 50.5 %all-to-all-start.2 = ((f32[4,1,4,32,256]{4,3,2,1,0:T(8,128)}), f32[4,1,4,32,256]{4,3,2,1,0:T(8,128)S(1)}, u32[]{:S(2)}, u32[]{:S(2)}) async-start(f32[4,1,4,32,256]{4,3,2,1,0:T(8,128)} %get-tuple-element.381), calls=%async_computation.2 | async-start | bytes 1048576 | tf_op jit(solution)/shard_map/all_to_all | solution.py:190
where the time goes:
time: 283 us; the launch traced here: 281 us
  starting transfers between devices  119 us (42%)
  blocking collectives  79.4 us (28%)
  other arithmetic  33.1 us (12%)
  waiting for transfers between devices  20.6 us (7%)
  matrix products  17.5 us (6%)
  local copies, waits for them, and re-layouts  7.58 us (3%)
  loops' own time  3.42 us (1%)
    ppermute x16, starting transfers between devices, padded(): lax.ppermute(tail, axis, [(i, (i + 1) % count) for i in range(ends)])  89.6 us
    psum x1, blocking collectives, body(): totals = lax.psum(misfit, ('tm', 'space'))  46.4 us
    ppermute x16, starting transfers between devices, padded(): lax.ppermute(head, axis, [((i + 1) % count, i) for i in range(ends)])  21.2 us
    ppermute x16, waiting for transfers between devices, padded(): lax.ppermute(tail, axis, [(i, (i + 1) % count) for i in range(ends)])  18.9 us
    dot_general x4, matrix products, mismatch(): jnp.dot(pressure.reshape(batch_size, -1), well_picks.T, precision=lax.Pre...  16.2 us
    all_to_all x1, blocking collectives, body(): lax.all_to_all(result[2], 'tm', split_axis=0, concat_axis=1, tiled=True)  12.3 us
    add x2, other arithmetic, region_fields(): summed + jnp.where(region_ids == region_index, region_table[table_row, re...  10.3 us
    all_gather x1, blocking collectives, body(): lax.all_gather(inflow, 'tm', axis=0, tiled=True)  8.19 us
  transfers between devices with their start and end apart: 34, of which 17 were waited for; matrix products, arithmetic and copies ran while one was open for 13% of the time, Pallas kernels for 0%

commit v1 on v0

--- a/solution.py
+++ b/solution.py
@@ -190,7 +190,8 @@
         lax.all_to_all(result[3], "tm", split_axis=0, concat_axis=1, tiled=True),
     )
     misfit = lax.dynamic_update_slice_in_dim(misfit, result[4], section_index * batch_size, 0)
-    totals = lax.psum(misfit, ("tm", "space"))
+    inner = lax.psum(misfit, "tm")
+    totals = lax.psum(inner, "space")
     return (totals / (sections * REP_DEV * well_cells.shape[0]), slab_pressure, slab_saturation)
 
 

time: 283 us -> 270 us (0.954)
  blocking collectives: 79.4 us -> 67.2 us
    psum x1 -> x2, blocking collectives: 46.4 us -> 34.2 us  [the longest x1 24 us: body(): totals = lax.psum(inner, 'space')]
  transfers between devices with their start and end apart: 34 -> 34, of which waited for: 17 -> 17; matrix products, arithmetic and copies ran while one was open for 13% -> 14% of each run, Pallas kernels for 0% -> 0%
where the time goes in v1:
time: 270 us; the launch traced here: 268 us
  starting transfers between devices  119 us (44%)
  blocking collectives  67.2 us (25%)
  other arithmetic  33.2 us (12%)
  waiting for transfers between devices  20.6 us (8%)
  matrix products  17.3 us (6%)
  local copies, waits for them, and re-layouts  7.57 us (3%)
  loops' own time  3.16 us (1%)
    ppermute x16, starting transfers between devices, padded(): lax.ppermute(tail, axis, [(i, (i + 1) % count) for i in range(ends)])  89.6 us
    psum x1, blocking collectives, body(): totals = lax.psum(inner, 'space')  24 us
    ppermute x16, starting transfers between devices, padded(): lax.ppermute(head, axis, [((i + 1) % count, i) for i in range(ends)])  21.2 us
    ppermute x16, waiting for transfers between devices, padded(): lax.ppermute(tail, axis, [(i, (i + 1) % count) for i in range(ends)])  18.9 us
    dot_general x4, matrix products, mismatch(): jnp.dot(pressure.reshape(batch_size, -1), well_picks.T, precision=lax.Pre...  16 us
    all_to_all x1, blocking collectives, body(): lax.all_to_all(result[2], 'tm', split_axis=0, concat_axis=1, tiled=True)  12.3 us
    add x2, other arithmetic, region_fields(): summed + jnp.where(region_ids == region_index, region_table[table_row, re...  10.3 us
    psum x1, blocking collectives, body(): inner = lax.psum(misfit, 'tm')  10.1 us
  transfers between devices with their start and end apart: 34, of which 17 were waited for; matrix products, arithmetic and copies ran while one was open for 14% of the time, Pallas kernels for 0%

profile of v1, /device:TPU:0, one launch (start us, length us, event | category | flops | bytes accessed | tf_op | source)
XLA Modules:
  0.0 268.5 jit_solution(4870686775482800667)
XLA Ops:
  0.7 4.4 %all-to-all-start = ((f32[4,1,32]{2,1,0:T(1,128)}), f32[4,1,32]{2,1,0:T(1,128)S(1)}, u32[]{:S(2)}, u32[]{:S(2)}) async-start(f32[4,1,32]{2,1,0:T(1,128)} %param.21), calls=%async_computation | async-start | bytes 4096 | tf_op jit(solution)/shard_map/all_to_all | solution.py:159
  6.6 5.2 %all-gather = f32[4,1,32]{2,1,0:T(1,128)S(1)} all-gather(f32[1,1,32]{2,1,0:T(1,128)S(1)} %bitcast.154), channel_id=1, replica_groups=mesh['tm'=4,'space'=8] {'tm'}, dimensions={0}, use_global_device_ids=true | all-gather | bytes 640 | tf_op jit(solution)/shard_map/all_gather | solution.py:157
  12.6 1.3 fusion.102
  13.9 8.2 %all_gather.10 = f32[4,4,32,256]{3,2,1,0:T(8,128)} all-gather(f32[1,4,32,256]{3,2,1,0:T(8,128)S(1)} %copy-done.7), channel_id=1, replica_groups=mesh['tm'=4,'space'=8] {'tm'}, dimensions={0}, use_global_device_ids=true | all-gather | bytes 655360 | tf_op jit(solution)/shard_map/all_gather | solution.py:156
  22.1 7.4 %all_gather.11 = f32[4,4,32,256]{3,2,1,0:T(8,128)S(1)} all-gather(f32[1,4,32,256]{3,2,1,0:T(8,128)S(1)} %copy-done.8), channel_id=1, replica_groups=mesh['tm'=4,'space'=8] {'tm'}, dimensions={0}, use_global_device_ids=true | all-gather | bytes 655360 | tf_op jit(solution)/shard_map/all_gather | solution.py:155
  29.6 5.2 %select_add_fusion = (f32[4,32,256]{2,1,0:T(8,128)S(1)}, pred[4,32,256]{2,1,0:T(8,128)(4,1)S(1)}, pred[4,32,256]{2,1,0:T(8,128)(4,1)S(1)}, pred[4,32,256]{2,1,0:...) fusion(f32[]{:T(128)} %bitcast.28, f32[]{:T(128)} %bitcast.27, ...), kind=kLoop, calls=%fused_computation.152 | loop fusion | flops 753664 | bytes 524320 | tf_op jit(solution)/shard_map/add | solution.py:96
  34.8 5.1 %add_multiply_fusion = f32[4,32,256]{2,1,0:T(8,128)S(1)} fusion(pred[4,32,256]{2,1,0:T(8,128)(4,1)S(1)} %get-tuple-element.474, pred[4,32,256]{2,1,0:T(8,128)(4,1)S(1)} %get-tuple-element.473, pred[4,32,256]{2,1,0:T(8,128)(4,1)S(1)} %get-tuple-element.472, pred[4,32,256]{2,1,0:T(8,128)(4,1)S(1)} %get-tuple-element.471, ...), kind=kLoop, calls=%fused_computation.153 | loop fusion | flops 524288 | bytes 393248 | tf_op jit(solution)/shard_map/mul | solution.py:100
  39.9 5.1 %select_add_fusion.1 = f32[4,32,256]{2,1,0:T(8,128)S(1)} fusion(pred[4,32,256]{2,1,0:T(8,128)(4,1)S(1)} %get-tuple-element.474, pred[4,32,256]{2,1,0:T(8,128)(4,1)S(1)} %get-tuple-element.473, pred[4,32,256]{2,1,0:T(8,128)(4,1)S(1)} %get-tuple-element.472, pred[4,32,256]{2,1,0:T(8,128)(4,1)S(1)} %get-tuple-element.471, ...), kind=kLoop, calls=%fused_computation.155 | loop fusion | flops 491520 | bytes 393248 | tf_op jit(solution)/shard_map/add | solution.py:96
  46.0 170.3 %while.24 = (s32[]{:T(128)}, f32[1,4,32,256]{3,2,1,0:T(8,128)S(1)}, f32[1,4,32,256]{3,2,1,0:T(8,128)S(1)}, f32[4,1,4,32,256]{4,3,2,1,0:T(8,128)}, f32[4,1,4,32,2...) while((s32[]{:T(128)}, f32[1,4,32,256]{3,2,1,0:T(8,128)S(1)}, ...), condition=%wide.region_3.4_spmd.clone, body=%wide.region_1.3_spmd.clone.sunk | while | flops 19529856 | bytes 16516069 | solution.py:182
  46.1 1.3 collective-permute-start
  47.4 4.5 %collective-permute-start.1 = (f32[2,1,1,32,256]{4,3,2,1,0:T(8,128)S(1)}, f32[2,1,1,32,256]{4,3,2,1,0:T(8,128)S(1)}, u32[]{:S(2)}, u32[]{:S(2)}) collective-permute-start(f32[2,1,1,32,256]{4,3,2,1,0:T(8,128)S(1)} %get-tuple-element.644), channel_id=1, source_target_pairs={{0,1},{1,2},{2,3},{3,4},{4,5},{5,6},{6,7},{8,9},{9,10},{10,11},{11... | collective-permute-start | bytes 196616 | tf_op jit(solution)/shard_map/while/body/eval_jaxpr/ppermute | solution.py:19
  52.5 1.6 collective-permute-done.1
  54.1 1.3 fusion.133
  55.4 1.3 collective-permute-start.2
  56.7 5.1 %collective-permute-start.3 = (f32[1,1,32,256]{3,2,1,0:T(8,128)S(1)}, f32[1,1,32,256]{3,2,1,0:T(8,128)S(1)}, u32[]{:S(2)}, u32[]{:S(2)}) collective-permute-start(f32[1,1,32,256]{3,2,1,0:T(8,128)S(1)} %get-tuple-element.656), channel_id=1, source_target_pairs={{0,1},{1,2},{2,3},{3,4},{4,5},{5,6},{6,7},{8,9},{9,10},{10,11},{11... | collective-permute-start | bytes 98312 | tf_op jit(solution)/shard_map/while/body/eval_jaxpr/ppermute | solution.py:19
  61.9 1.6 collective-permute-done.3
  63.6 1.3 collective-permute-start.4
  64.9 5.8 %collective-permute-start.5 = (f32[1,1,32,256]{3,2,1,0:T(8,128)S(1)}, f32[1,1,32,256]{3,2,1,0:T(8,128)S(1)}, u32[]{:S(2)}, u32[]{:S(2)}) collective-permute-start(f32[1,1,32,256]{3,2,1,0:T(8,128)S(1)} %get-tuple-element.658), channel_id=1, source_target_pairs={{0,1},{1,2},{2,3},{3,4},{4,5},{5,6},{6,7},{8,9},{9,10},{10,11},{11... | collective-permute-start | bytes 98312 | tf_op jit(solution)/shard_map/while/body/eval_jaxpr/ppermute | solution.py:19
  70.7 1.6 collective-permute-done.5
  72.9 1.6 constant_dynamic-update-slice_fusion.2
  74.5 1.4 collective-permute-start.6
  75.9 5.8 %collective-permute-start.7 = (f32[2,1,1,32,256]{4,3,2,1,0:T(8,128)S(1)}, f32[2,1,1,32,256]{4,3,2,1,0:T(8,128)S(1)}, u32[]{:S(2)}, u32[]{:S(2)}) collective-permute-start(f32[2,1,1,32,256]{4,3,2,1,0:T(8,128)S(1)} %get-tuple-element.662), channel_id=1, source_target_pairs={{0,1},{1,2},{2,3},{3,4},{4,5},{5,6},{6,7},{8,9},{9,10},{10,11},{11... | collective-permute-start | bytes 196616 | tf_op jit(solution)/shard_map/while/body/eval_jaxpr/ppermute | solution.py:19
  81.8 4.0 %fusion.137 = f32[]{:T(128)} fusion(f32[32]{0:T(128)S(1)} %get-tuple-element.718, f32[32768,1]{0,1:T(1,128)S(1)} %bitcast.144, s32[32768]{0:T(1024)S(1)} %copy-done.6, s32[32]{0:T(128)S(1)} %get-tuple-element.720, f32[1,4,32]{2,1,0:T(4,128)S(1)} %get-tuple-element.717, s32[]{:T(128)S(6)} %copy.28), kind=kOutput, calls=%fused_computation.10.clone.1 | convolution fusion | flops 14680191 | bytes 262536 | tf_op jit(solution)/shard_map/while/body/eval_jaxpr/dot_general | solution.py:148
  88.8 5.8 %collective-permute-start.1 = (f32[2,1,1,32,256]{4,3,2,1,0:T(8,128)S(1)}, f32[2,1,1,32,256]{4,3,2,1,0:T(8,128)S(1)}, u32[]{:S(2)}, u32[]{:S(2)}) collective-permute-start(f32[2,1,1,32,256]{4,3,2,1,0:T(8,128)S(1)} %get-tuple-element.644), channel_id=1, source_target_pairs={{0,1},{1,2},{2,3},{3,4},{4,5},{5,6},{6,7},{8,9},{9,10},{10,11},{11... | collective-permute-start | bytes 196616 | tf_op jit(solution)/shard_map/while/body/eval_jaxpr/ppermute | solution.py:19
  94.9 1.6 collective-permute-done.1
  96.6 1.3 fusion.133
  97.9 1.3 collective-permute-start.2
  99.2 5.4 %collective-permute-start.3 = (f32[1,1,32,256]{3,2,1,0:T(8,128)S(1)}, f32[1,1,32,256]{3,2,1,0:T(8,128)S(1)}, u32[]{:S(2)}, u32[]{:S(2)}) collective-permute-start(f32[1,1,32,256]{3,2,1,0:T(8,128)S(1)} %get-tuple-element.656), channel_id=1, source_target_pairs={{0,1},{1,2},{2,3},{3,4},{4,5},{5,6},{6,7},{8,9},{9,10},{10,11},{11... | collective-permute-start | bytes 98312 | tf_op jit(solution)/shard_map/while/body/eval_jaxpr/ppermute | solution.py:19
  104.7 1.6 collective-permute-done.3
  106.4 1.3 collective-permute-start.4
  107.7 5.8 %collective-permute-start.5 = (f32[1,1,32,256]{3,2,1,0:T(8,128)S(1)}, f32[1,1,32,256]{3,2,1,0:T(8,128)S(1)}, u32[]{:S(2)}, u32[]{:S(2)}) collective-permute-start(f32[1,1,32,256]{3,2,1,0:T(8,128)S(1)} %get-tuple-element.658), channel_id=1, source_target_pairs={{0,1},{1,2},{2,3},{3,4},{4,5},{5,6},{6,7},{8,9},{9,10},{10,11},{11... | collective-permute-start | bytes 98312 | tf_op jit(solution)/shard_map/while/body/eval_jaxpr/ppermute | solution.py:19
  113.5 1.6 collective-permute-done.5
  115.7 1.6 constant_dynamic-update-slice_fusion.2
  117.3 1.4 collective-permute-start.6
  118.7 5.8 %collective-permute-start.7 = (f32[2,1,1,32,256]{4,3,2,1,0:T(8,128)S(1)}, f32[2,1,1,32,256]{4,3,2,1,0:T(8,128)S(1)}, u32[]{:S(2)}, u32[]{:S(2)}) collective-permute-start(f32[2,1,1,32,256]{4,3,2,1,0:T(8,128)S(1)} %get-tuple-element.662), channel_id=1, source_target_pairs={{0,1},{1,2},{2,3},{3,4},{4,5},{5,6},{6,7},{8,9},{9,10},{10,11},{11... | collective-permute-start | bytes 196616 | tf_op jit(solution)/shard_map/while/body/eval_jaxpr/ppermute | solution.py:19
  124.6 4.0 %fusion.137 = f32[]{:T(128)} fusion(f32[32]{0:T(128)S(1)} %get-tuple-element.718, f32[32768,1]{0,1:T(1,128)S(1)} %bitcast.144, s32[32768]{0:T(1024)S(1)} %copy-done.6, s32[32]{0:T(128)S(1)} %get-tuple-element.720, f32[1,4,32]{2,1,0:T(4,128)S(1)} %get-tuple-element.717, s32[]{:T(128)S(6)} %copy.28), kind=kOutput, calls=%fused_computation.10.clone.1 | convolution fusion | flops 14680191 | bytes 262536 | tf_op jit(solution)/shard_map/while/body/eval_jaxpr/dot_general | solution.py:148
  131.7 5.9 %collective-permute-start.1 = (f32[2,1,1,32,256]{4,3,2,1,0:T(8,128)S(1)}, f32[2,1,1,32,256]{4,3,2,1,0:T(8,128)S(1)}, u32[]{:S(2)}, u32[]{:S(2)}) collective-permute-start(f32[2,1,1,32,256]{4,3,2,1,0:T(8,128)S(1)} %get-tuple-element.644), channel_id=1, source_target_pairs={{0,1},{1,2},{2,3},{3,4},{4,5},{5,6},{6,7},{8,9},{9,10},{10,11},{11... | collective-permute-start | bytes 196616 | tf_op jit(solution)/shard_map/while/body/eval_jaxpr/ppermute | solution.py:19
  137.9 1.7 collective-permute-done.1
  139.8 1.3 fusion.133
  141.1 1.3 collective-permute-start.2
  142.4 5.4 %collective-permute-start.3 = (f32[1,1,32,256]{3,2,1,0:T(8,128)S(1)}, f32[1,1,32,256]{3,2,1,0:T(8,128)S(1)}, u32[]{:S(2)}, u32[]{:S(2)}) collective-permute-start(f32[1,1,32,256]{3,2,1,0:T(8,128)S(1)} %get-tuple-element.656), channel_id=1, source_target_pairs={{0,1},{1,2},{2,3},{3,4},{4,5},{5,6},{6,7},{8,9},{9,10},{10,11},{11... | collective-permute-start | bytes 98312 | tf_op jit(solution)/shard_map/while/body/eval_jaxpr/ppermute | solution.py:19
  147.8 1.6 collective-permute-done.3
  150.9 5.9 %collective-permute-start.5 = (f32[1,1,32,256]{3,2,1,0:T(8,128)S(1)}, f32[1,1,32,256]{3,2,1,0:T(8,128)S(1)}, u32[]{:S(2)}, u32[]{:S(2)}) collective-permute-start(f32[1,1,32,256]{3,2,1,0:T(8,128)S(1)} %get-tuple-element.658), channel_id=1, source_target_pairs={{0,1},{1,2},{2,3},{3,4},{4,5},{5,6},{6,7},{8,9},{9,10},{10,11},{11... | collective-permute-start | bytes 98312 | tf_op jit(solution)/shard_map/while/body/eval_jaxpr/ppermute | solution.py:19
  156.9 1.5 collective-permute-done.5
  159.0 1.6 constant_dynamic-update-slice_fusion.2
  160.6 1.4 collective-permute-start.6
  162.1 5.7 %collective-permute-start.7 = (f32[2,1,1,32,256]{4,3,2,1,0:T(8,128)S(1)}, f32[2,1,1,32,256]{4,3,2,1,0:T(8,128)S(1)}, u32[]{:S(2)}, u32[]{:S(2)}) collective-permute-start(f32[2,1,1,32,256]{4,3,2,1,0:T(8,128)S(1)} %get-tuple-element.662), channel_id=1, source_target_pairs={{0,1},{1,2},{2,3},{3,4},{4,5},{5,6},{6,7},{8,9},{9,10},{10,11},{11... | collective-permute-start | bytes 196616 | tf_op jit(solution)/shard_map/while/body/eval_jaxpr/ppermute | solution.py:19
  167.9 4.0 %fusion.137 = f32[]{:T(128)} fusion(f32[32]{0:T(128)S(1)} %get-tuple-element.718, f32[32768,1]{0,1:T(1,128)S(1)} %bitcast.144, s32[32768]{0:T(1024)S(1)} %copy-done.6, s32[32]{0:T(128)S(1)} %get-tuple-element.720, f32[1,4,32]{2,1,0:T(4,128)S(1)} %get-tuple-element.717, s32[]{:T(128)S(6)} %copy.28), kind=kOutput, calls=%fused_computation.10.clone.1 | convolution fusion | flops 14680191 | bytes 262536 | tf_op jit(solution)/shard_map/while/body/eval_jaxpr/dot_general | solution.py:148
  173.6 1.3 collective-permute-start
  174.9 5.8 %collective-permute-start.1 = (f32[2,1,1,32,256]{4,3,2,1,0:T(8,128)S(1)}, f32[2,1,1,32,256]{4,3,2,1,0:T(8,128)S(1)}, u32[]{:S(2)}, u32[]{:S(2)}) collective-permute-start(f32[2,1,1,32,256]{4,3,2,1,0:T(8,128)S(1)} %get-tuple-element.644), channel_id=1, source_target_pairs={{0,1},{1,2},{2,3},{3,4},{4,5},{5,6},{6,7},{8,9},{9,10},{10,11},{11... | collective-permute-start | bytes 196616 | tf_op jit(solution)/shard_map/while/body/eval_jaxpr/ppermute | solution.py:19
  181.0 1.6 collective-permute-done.1
  182.7 1.3 fusion.133
  185.3 5.4 %collective-permute-start.3 = (f32[1,1,32,256]{3,2,1,0:T(8,128)S(1)}, f32[1,1,32,256]{3,2,1,0:T(8,128)S(1)}, u32[]{:S(2)}, u32[]{:S(2)}) collective-permute-start(f32[1,1,32,256]{3,2,1,0:T(8,128)S(1)} %get-tuple-element.656), channel_id=1, source_target_pairs={{0,1},{1,2},{2,3},{3,4},{4,5},{5,6},{6,7},{8,9},{9,10},{10,11},{11... | collective-permute-start | bytes 98312 | tf_op jit(solution)/shard_map/while/body/eval_jaxpr/ppermute | solution.py:19
  190.7 1.6 collective-permute-done.3
  193.8 5.8 %collective-permute-start.5 = (f32[1,1,32,256]{3,2,1,0:T(8,128)S(1)}, f32[1,1,32,256]{3,2,1,0:T(8,128)S(1)}, u32[]{:S(2)}, u32[]{:S(2)}) collective-permute-start(f32[1,1,32,256]{3,2,1,0:T(8,128)S(1)} %get-tuple-element.658), channel_id=1, source_target_pairs={{0,1},{1,2},{2,3},{3,4},{4,5},{5,6},{6,7},{8,9},{9,10},{10,11},{11... | collective-permute-start | bytes 98312 | tf_op jit(solution)/shard_map/while/body/eval_jaxpr/ppermute | solution.py:19
  199.6 1.6 collective-permute-done.5
  201.8 1.6 constant_dynamic-update-slice_fusion.2
  203.3 1.4 collective-permute-start.6
  204.8 5.8 %collective-permute-start.7 = (f32[2,1,1,32,256]{4,3,2,1,0:T(8,128)S(1)}, f32[2,1,1,32,256]{4,3,2,1,0:T(8,128)S(1)}, u32[]{:S(2)}, u32[]{:S(2)}) collective-permute-start(f32[2,1,1,32,256]{4,3,2,1,0:T(8,128)S(1)} %get-tuple-element.662), channel_id=1, source_target_pairs={{0,1},{1,2},{2,3},{3,4},{4,5},{5,6},{6,7},{8,9},{9,10},{10,11},{11... | collective-permute-start | bytes 196616 | tf_op jit(solution)/shard_map/while/body/eval_jaxpr/ppermute | solution.py:19
  210.7 4.0 %fusion.137 = f32[]{:T(128)} fusion(f32[32]{0:T(128)S(1)} %get-tuple-element.718, f32[32768,1]{0,1:T(1,128)S(1)} %bitcast.144, s32[32768]{0:T(1024)S(1)} %copy-done.6, s32[32]{0:T(128)S(1)} %get-tuple-element.720, f32[1,4,32]{2,1,0:T(4,128)S(1)} %get-tuple-element.717, s32[]{:T(128)S(6)} %copy.28), kind=kOutput, calls=%fused_computation.10.clone.1 | convolution fusion | flops 14680191 | bytes 262536 | tf_op jit(solution)/shard_map/while/body/eval_jaxpr/dot_general | solution.py:148
  216.3 12.3 %all_to_all.36 = f32[4,1,4,32,256]{4,3,2,1,0:T(8,128)S(1)} all-to-all(f32[4,1,4,32,256]{4,3,2,1,0:T(8,128)} %get-tuple-element.380), channel_id=1, replica_groups=mesh['tm'=4,'space'=8] {'tm'}, dimensions={0} | all-to-all | bytes 1048576 | tf_op jit(solution)/shard_map/all_to_all | solution.py:189
  228.6 3.5 %all-to-all-start.2 = ((f32[4,1,4,32,256]{4,3,2,1,0:T(8,128)}), f32[4,1,4,32,256]{4,3,2,1,0:T(8,128)S(1)}, u32[]{:S(2)}, u32[]{:S(2)}) async-start(f32[4,1,4,32,256]{4,3,2,1,0:T(8,128)} %get-tuple-element.381), calls=%async_computation.2 | async-start | bytes 1048576 | tf_op jit(solution)/shard_map/all_to_all | solution.py:190
  232.2 10.1 %psum.14 = f32[4]{0:T(128)S(1)} all-reduce(f32[4]{0:T(128)S(1)} %dynamic_update_slice.24), channel_id=1, replica_groups=mesh['tm'=4,'space'=8] {'tm'}, use_global_device_ids=true, to_apply=%region_4.5 | all-reduce | flops 4 | bytes 32 | tf_op jit(solution)/shard_map/psum | solution.py:193
  242.3 24.0 %psum.15 = f32[4]{0:T(128)S(1)} all-reduce(f32[4]{0:T(128)S(1)} %psum.14), channel_id=1, replica_groups=mesh['tm'=4,'space'=8] {'space'}, use_global_device_ids=true, to_apply=%region_5.6 | all-reduce | flops 4 | bytes 32 | tf_op jit(solution)/shard_map/psum | solution.py:194
  (150 shorter events, 22.0 us)
Async XLA Ops:
  0.6 28.9 %copy-start = (f32[4,4,32,256]{3,2,1,0:T(8,128)S(1)}, f32[4,4,32,256]{3,2,1,0:T(8,128)}, u32[]{:S(2)}) copy-start(f32[4,4,32,256]{3,2,1,0:T(8,128)} %param.12) | copy-start | bytes 1572868
  0.6 4.4 %copy-start.10 = (f32[3,8]{1,0:T(4,128)S(1)}, f32[3,8]{1,0:T(4,128)}, u32[]{:S(2)}) copy-start(f32[3,8]{1,0:T(4,128)} %param.18) | copy-start | bytes 292
  0.7 11.1 %copy-start.11 = (s32[32]{0:T(128)S(1)}, s32[32]{0:T(128)}, u32[]{:S(2)}) copy-start(s32[32]{0:T(128)} %param.19) | copy-start | bytes 388
  0.7 6.0 %copy-start.12 = (f32[1,32]{1,0:T(1,128)S(1)}, f32[1,32]{1,0:T(1,128)}, u32[]{:S(2)}) copy-start(f32[1,32]{1,0:T(1,128)} %param.20) | copy-start | bytes 388
  0.7 44.5 %all-to-all-start = ((f32[4,1,32]{2,1,0:T(1,128)}), f32[4,1,32]{2,1,0:T(1,128)S(1)}, u32[]{:S(2)}, u32[]{:S(2)}) async-start(f32[4,1,32]{2,1,0:T(1,128)} %param.21), calls=%async_computation | async-start | bytes 4096 | tf_op jit(solution)/shard_map/all_to_all | solution.py:159
  6.6 7.3 %copy-start.5 = (s32[16,2,8,128]{3,1,2,0:T(2,128)}, s32[16,2,8,128]{3,1,2,0:T(2,128)S(1)}, u32[]{:S(2)}) copy-start(s32[16,2,8,128]{3,1,2,0:T(2,128)S(1)} %copy.16) | copy-start | bytes 393220
  12.6 1.4 copy-start.7
  13.9 8.2 %copy-start.8 = (f32[1,4,32,256]{3,2,1,0:T(8,128)S(1)}, f32[1,4,32,256]{3,2,1,0:T(8,128)}, u32[]{:S(2)}) copy-start(f32[1,4,32,256]{3,2,1,0:T(8,128)} %param.13) | copy-start | bytes 393220
  22.1 7.4 %copy-start.9 = (s32[4,32,256]{2,1,0:T(8,128)S(1)}, s32[4,32,256]{2,1,0:T(8,128)}, u32[]{:S(2)}) copy-start(s32[4,32,256]{2,1,0:T(8,128)} %param.17) | copy-start | bytes 393220
  45.0 0.9 copy-start.1
  45.0 1.0 copy-start.2
  46.1 6.4 %collective-permute-start = (f32[2,1,1,32,256]{4,3,2,1,0:T(8,128)S(1)}, f32[2,1,1,32,256]{4,3,2,1,0:T(8,128)S(1)}, u32[]{:S(2)}, u32[]{:S(2)}) collective-permute-start(f32[2,1,1,32,256]{4,3,2,1,0:T(8,128)S(1)} %get-tuple-element.643), channel_id=1, source_target_pairs={{1,0},{2,1},{3,2},{4,3},{5,4},{6,5},{7,6},{9,8},{10,9},{11,10},{12... | collective-permute-start | bytes 196616 | tf_op jit(solution)/shard_map/while/body/eval_jaxpr/ppermute | solution.py:21
  47.4 6.7 %collective-permute-start.1 = (f32[2,1,1,32,256]{4,3,2,1,0:T(8,128)S(1)}, f32[2,1,1,32,256]{4,3,2,1,0:T(8,128)S(1)}, u32[]{:S(2)}, u32[]{:S(2)}) collective-permute-start(f32[2,1,1,32,256]{4,3,2,1,0:T(8,128)S(1)} %get-tuple-element.644), channel_id=1, source_target_pairs={{0,1},{1,2},{2,3},{3,4},{4,5},{5,6},{6,7},{8,9},{9,10},{10,11},{11... | collective-permute-start | bytes 196616 | tf_op jit(solution)/shard_map/while/body/eval_jaxpr/ppermute | solution.py:19
  55.4 6.4 %collective-permute-start.2 = (f32[1,1,32,256]{3,2,1,0:T(8,128)S(1)}, f32[1,1,32,256]{3,2,1,0:T(8,128)S(1)}, u32[]{:S(2)}, u32[]{:S(2)}) collective-permute-start(f32[1,1,32,256]{3,2,1,0:T(8,128)S(1)} %get-tuple-element.655), channel_id=1, source_target_pairs={{1,0},{2,1},{3,2},{4,3},{5,4},{6,5},{7,6},{9,8},{10,9},{11,10},{12... | collective-permute-start | bytes 98312 | tf_op jit(solution)/shard_map/while/body/eval_jaxpr/ppermute | solution.py:21
  56.7 6.7 %collective-permute-start.3 = (f32[1,1,32,256]{3,2,1,0:T(8,128)S(1)}, f32[1,1,32,256]{3,2,1,0:T(8,128)S(1)}, u32[]{:S(2)}, u32[]{:S(2)}) collective-permute-start(f32[1,1,32,256]{3,2,1,0:T(8,128)S(1)} %get-tuple-element.656), channel_id=1, source_target_pairs={{0,1},{1,2},{2,3},{3,4},{4,5},{5,6},{6,7},{8,9},{9,10},{10,11},{11... | collective-permute-start | bytes 98312 | tf_op jit(solution)/shard_map/while/body/eval_jaxpr/ppermute | solution.py:19
  63.6 7.1 %collective-permute-start.4 = (f32[1,1,32,256]{3,2,1,0:T(8,128)S(1)}, f32[1,1,32,256]{3,2,1,0:T(8,128)S(1)}, u32[]{:S(2)}, u32[]{:S(2)}) collective-permute-start(f32[1,1,32,256]{3,2,1,0:T(8,128)S(1)} %get-tuple-element.657), channel_id=1, source_target_pairs={{1,0},{2,1},{3,2},{4,3},{5,4},{6,5},{7,6},{9,8},{10,9},{11,10},{12... | collective-permute-start | bytes 98312 | tf_op jit(solution)/shard_map/while/body/eval_jaxpr/ppermute | solution.py:21
  64.9 7.4 %collective-permute-start.5 = (f32[1,1,32,256]{3,2,1,0:T(8,128)S(1)}, f32[1,1,32,256]{3,2,1,0:T(8,128)S(1)}, u32[]{:S(2)}, u32[]{:S(2)}) collective-permute-start(f32[1,1,32,256]{3,2,1,0:T(8,128)S(1)} %get-tuple-element.658), channel_id=1, source_target_pairs={{0,1},{1,2},{2,3},{3,4},{4,5},{5,6},{6,7},{8,9},{9,10},{10,11},{11... | collective-permute-start | bytes 98312 | tf_op jit(solution)/shard_map/while/body/eval_jaxpr/ppermute | solution.py:19
  70.7 1.6 copy-start.3
  72.3 0.6 copy-start.4
  74.5 7.4 %copy-start.6 = (s32[32768]{0:T(1024)S(1)}, s32[32768]{0:T(1024)}, u32[]{:S(2)}) copy-start(s32[32768]{0:T(1024)} %get-tuple-element.719) | copy-start | bytes 393220 | tf_op jit(solution)/shard_map/while
  74.5 11.9 %collective-permute-start.6 = (f32[2,1,1,32,256]{4,3,2,1,0:T(8,128)S(1)}, f32[2,1,1,32,256]{4,3,2,1,0:T(8,128)S(1)}, u32[]{:S(2)}, u32[]{:S(2)}) collective-permute-start(f32[2,1,1,32,256]{4,3,2,1,0:T(8,128)S(1)} %get-tuple-element.661), channel_id=1, source_target_pairs={{1,0},{2,1},{3,2},{4,3},{5,4},{6,5},{7,6},{9,8},{10,9},{11,10},{12... | collective-permute-start | bytes 196616 | tf_op jit(solution)/shard_map/while/body/eval_jaxpr/ppermute | solution.py:21
  75.9 10.5 %collective-permute-start.7 = (f32[2,1,1,32,256]{4,3,2,1,0:T(8,128)S(1)}, f32[2,1,1,32,256]{4,3,2,1,0:T(8,128)S(1)}, u32[]{:S(2)}, u32[]{:S(2)}) collective-permute-start(f32[2,1,1,32,256]{4,3,2,1,0:T(8,128)S(1)} %get-tuple-element.662), channel_id=1, source_target_pairs={{0,1},{1,2},{2,3},{3,4},{4,5},{5,6},{6,7},{8,9},{9,10},{10,11},{11... | collective-permute-start | bytes 196616 | tf_op jit(solution)/shard_map/while/body/eval_jaxpr/ppermute | solution.py:19
  87.5 7.4 %collective-permute-start = (f32[2,1,1,32,256]{4,3,2,1,0:T(8,128)S(1)}, f32[2,1,1,32,256]{4,3,2,1,0:T(8,128)S(1)}, u32[]{:S(2)}, u32[]{:S(2)}) collective-permute-start(f32[2,1,1,32,256]{4,3,2,1,0:T(8,128)S(1)} %get-tuple-element.643), channel_id=1, source_target_pairs={{1,0},{2,1},{3,2},{4,3},{5,4},{6,5},{7,6},{9,8},{10,9},{11,10},{12... | collective-permute-start | bytes 196616 | tf_op jit(solution)/shard_map/while/body/eval_jaxpr/ppermute | solution.py:21
  88.8 7.6 %collective-permute-start.1 = (f32[2,1,1,32,256]{4,3,2,1,0:T(8,128)S(1)}, f32[2,1,1,32,256]{4,3,2,1,0:T(8,128)S(1)}, u32[]{:S(2)}, u32[]{:S(2)}) collective-permute-start(f32[2,1,1,32,256]{4,3,2,1,0:T(8,128)S(1)} %get-tuple-element.644), channel_id=1, source_target_pairs={{0,1},{1,2},{2,3},{3,4},{4,5},{5,6},{6,7},{8,9},{9,10},{10,11},{11... | collective-permute-start | bytes 196616 | tf_op jit(solution)/shard_map/while/body/eval_jaxpr/ppermute | solution.py:19
  97.9 6.8 %collective-permute-start.2 = (f32[1,1,32,256]{3,2,1,0:T(8,128)S(1)}, f32[1,1,32,256]{3,2,1,0:T(8,128)S(1)}, u32[]{:S(2)}, u32[]{:S(2)}) collective-permute-start(f32[1,1,32,256]{3,2,1,0:T(8,128)S(1)} %get-tuple-element.655), channel_id=1, source_target_pairs={{1,0},{2,1},{3,2},{4,3},{5,4},{6,5},{7,6},{9,8},{10,9},{11,10},{12... | collective-permute-start | bytes 98312 | tf_op jit(solution)/shard_map/while/body/eval_jaxpr/ppermute | solution.py:21
  99.2 7.0 %collective-permute-start.3 = (f32[1,1,32,256]{3,2,1,0:T(8,128)S(1)}, f32[1,1,32,256]{3,2,1,0:T(8,128)S(1)}, u32[]{:S(2)}, u32[]{:S(2)}) collective-permute-start(f32[1,1,32,256]{3,2,1,0:T(8,128)S(1)} %get-tuple-element.656), channel_id=1, source_target_pairs={{0,1},{1,2},{2,3},{3,4},{4,5},{5,6},{6,7},{8,9},{9,10},{10,11},{11... | collective-permute-start | bytes 98312 | tf_op jit(solution)/shard_map/while/body/eval_jaxpr/ppermute | solution.py:19
  106.4 7.1 %collective-permute-start.4 = (f32[1,1,32,256]{3,2,1,0:T(8,128)S(1)}, f32[1,1,32,256]{3,2,1,0:T(8,128)S(1)}, u32[]{:S(2)}, u32[]{:S(2)}) collective-permute-start(f32[1,1,32,256]{3,2,1,0:T(8,128)S(1)} %get-tuple-element.657), channel_id=1, source_target_pairs={{1,0},{2,1},{3,2},{4,3},{5,4},{6,5},{7,6},{9,8},{10,9},{11,10},{12... | collective-permute-start | bytes 98312 | tf_op jit(solution)/shard_map/while/body/eval_jaxpr/ppermute | solution.py:21
  107.7 7.4 %collective-permute-start.5 = (f32[1,1,32,256]{3,2,1,0:T(8,128)S(1)}, f32[1,1,32,256]{3,2,1,0:T(8,128)S(1)}, u32[]{:S(2)}, u32[]{:S(2)}) collective-permute-start(f32[1,1,32,256]{3,2,1,0:T(8,128)S(1)} %get-tuple-element.658), channel_id=1, source_target_pairs={{0,1},{1,2},{2,3},{3,4},{4,5},{5,6},{6,7},{8,9},{9,10},{10,11},{11... | collective-permute-start | bytes 98312 | tf_op jit(solution)/shard_map/while/body/eval_jaxpr/ppermute | solution.py:19
  113.5 1.6 copy-start.3
  115.1 0.6 copy-start.4
  117.3 7.4 %copy-start.6 = (s32[32768]{0:T(1024)S(1)}, s32[32768]{0:T(1024)}, u32[]{:S(2)}) copy-start(s32[32768]{0:T(1024)} %get-tuple-element.719) | copy-start | bytes 393220 | tf_op jit(solution)/shard_map/while
  117.3 11.9 %collective-permute-start.6 = (f32[2,1,1,32,256]{4,3,2,1,0:T(8,128)S(1)}, f32[2,1,1,32,256]{4,3,2,1,0:T(8,128)S(1)}, u32[]{:S(2)}, u32[]{:S(2)}) collective-permute-start(f32[2,1,1,32,256]{4,3,2,1,0:T(8,128)S(1)} %get-tuple-element.661), channel_id=1, source_target_pairs={{1,0},{2,1},{3,2},{4,3},{5,4},{6,5},{7,6},{9,8},{10,9},{11,10},{12... | collective-permute-start | bytes 196616 | tf_op jit(solution)/shard_map/while/body/eval_jaxpr/ppermute | solution.py:21
  118.7 10.5 %collective-permute-start.7 = (f32[2,1,1,32,256]{4,3,2,1,0:T(8,128)S(1)}, f32[2,1,1,32,256]{4,3,2,1,0:T(8,128)S(1)}, u32[]{:S(2)}, u32[]{:S(2)}) collective-permute-start(f32[2,1,1,32,256]{4,3,2,1,0:T(8,128)S(1)} %get-tuple-element.662), channel_id=1, source_target_pairs={{0,1},{1,2},{2,3},{3,4},{4,5},{5,6},{6,7},{8,9},{9,10},{10,11},{11... | collective-permute-start | bytes 196616 | tf_op jit(solution)/shard_map/while/body/eval_jaxpr/ppermute | solution.py:19
  130.3 7.6 %collective-permute-start = (f32[2,1,1,32,256]{4,3,2,1,0:T(8,128)S(1)}, f32[2,1,1,32,256]{4,3,2,1,0:T(8,128)S(1)}, u32[]{:S(2)}, u32[]{:S(2)}) collective-permute-start(f32[2,1,1,32,256]{4,3,2,1,0:T(8,128)S(1)} %get-tuple-element.643), channel_id=1, source_target_pairs={{1,0},{2,1},{3,2},{4,3},{5,4},{6,5},{7,6},{9,8},{10,9},{11,10},{12... | collective-permute-start | bytes 196616 | tf_op jit(solution)/shard_map/while/body/eval_jaxpr/ppermute | solution.py:21
  131.7 8.0 %collective-permute-start.1 = (f32[2,1,1,32,256]{4,3,2,1,0:T(8,128)S(1)}, f32[2,1,1,32,256]{4,3,2,1,0:T(8,128)S(1)}, u32[]{:S(2)}, u32[]{:S(2)}) collective-permute-start(f32[2,1,1,32,256]{4,3,2,1,0:T(8,128)S(1)} %get-tuple-element.644), channel_id=1, source_target_pairs={{0,1},{1,2},{2,3},{3,4},{4,5},{5,6},{6,7},{8,9},{9,10},{10,11},{11... | collective-permute-start | bytes 196616 | tf_op jit(solution)/shard_map/while/body/eval_jaxpr/ppermute | solution.py:19
  141.1 6.7 %collective-permute-start.2 = (f32[1,1,32,256]{3,2,1,0:T(8,128)S(1)}, f32[1,1,32,256]{3,2,1,0:T(8,128)S(1)}, u32[]{:S(2)}, u32[]{:S(2)}) collective-permute-start(f32[1,1,32,256]{3,2,1,0:T(8,128)S(1)} %get-tuple-element.655), channel_id=1, source_target_pairs={{1,0},{2,1},{3,2},{4,3},{5,4},{6,5},{7,6},{9,8},{10,9},{11,10},{12... | collective-permute-start | bytes 98312 | tf_op jit(solution)/shard_map/while/body/eval_jaxpr/ppermute | solution.py:21
  142.4 7.0 %collective-permute-start.3 = (f32[1,1,32,256]{3,2,1,0:T(8,128)S(1)}, f32[1,1,32,256]{3,2,1,0:T(8,128)S(1)}, u32[]{:S(2)}, u32[]{:S(2)}) collective-permute-start(f32[1,1,32,256]{3,2,1,0:T(8,128)S(1)} %get-tuple-element.656), channel_id=1, source_target_pairs={{0,1},{1,2},{2,3},{3,4},{4,5},{5,6},{6,7},{8,9},{9,10},{10,11},{11... | collective-permute-start | bytes 98312 | tf_op jit(solution)/shard_map/while/body/eval_jaxpr/ppermute | solution.py:19
  149.6 7.3 %collective-permute-start.4 = (f32[1,1,32,256]{3,2,1,0:T(8,128)S(1)}, f32[1,1,32,256]{3,2,1,0:T(8,128)S(1)}, u32[]{:S(2)}, u32[]{:S(2)}) collective-permute-start(f32[1,1,32,256]{3,2,1,0:T(8,128)S(1)} %get-tuple-element.657), channel_id=1, source_target_pairs={{1,0},{2,1},{3,2},{4,3},{5,4},{6,5},{7,6},{9,8},{10,9},{11,10},{12... | collective-permute-start | bytes 98312 | tf_op jit(solution)/shard_map/while/body/eval_jaxpr/ppermute | solution.py:21
  150.9 7.6 %collective-permute-start.5 = (f32[1,1,32,256]{3,2,1,0:T(8,128)S(1)}, f32[1,1,32,256]{3,2,1,0:T(8,128)S(1)}, u32[]{:S(2)}, u32[]{:S(2)}) collective-permute-start(f32[1,1,32,256]{3,2,1,0:T(8,128)S(1)} %get-tuple-element.658), channel_id=1, source_target_pairs={{0,1},{1,2},{2,3},{3,4},{4,5},{5,6},{6,7},{8,9},{9,10},{10,11},{11... | collective-permute-start | bytes 98312 | tf_op jit(solution)/shard_map/while/body/eval_jaxpr/ppermute | solution.py:19
  156.9 1.5 copy-start.3
  158.4 0.6 copy-start.4
  160.6 7.3 %copy-start.6 = (s32[32768]{0:T(1024)S(1)}, s32[32768]{0:T(1024)}, u32[]{:S(2)}) copy-start(s32[32768]{0:T(1024)} %get-tuple-element.719) | copy-start | bytes 393220 | tf_op jit(solution)/shard_map/while
  160.6 11.8 %collective-permute-start.6 = (f32[2,1,1,32,256]{4,3,2,1,0:T(8,128)S(1)}, f32[2,1,1,32,256]{4,3,2,1,0:T(8,128)S(1)}, u32[]{:S(2)}, u32[]{:S(2)}) collective-permute-start(f32[2,1,1,32,256]{4,3,2,1,0:T(8,128)S(1)} %get-tuple-element.661), channel_id=1, source_target_pairs={{1,0},{2,1},{3,2},{4,3},{5,4},{6,5},{7,6},{9,8},{10,9},{11,10},{12... | collective-permute-start | bytes 196616 | tf_op jit(solution)/shard_map/while/body/eval_jaxpr/ppermute | solution.py:21
  162.1 10.4 %collective-permute-start.7 = (f32[2,1,1,32,256]{4,3,2,1,0:T(8,128)S(1)}, f32[2,1,1,32,256]{4,3,2,1,0:T(8,128)S(1)}, u32[]{:S(2)}, u32[]{:S(2)}) collective-permute-start(f32[2,1,1,32,256]{4,3,2,1,0:T(8,128)S(1)} %get-tuple-element.662), channel_id=1, source_target_pairs={{0,1},{1,2},{2,3},{3,4},{4,5},{5,6},{6,7},{8,9},{9,10},{10,11},{11... | collective-permute-start | bytes 196616 | tf_op jit(solution)/shard_map/while/body/eval_jaxpr/ppermute | solution.py:19
  173.6 7.4 %collective-permute-start = (f32[2,1,1,32,256]{4,3,2,1,0:T(8,128)S(1)}, f32[2,1,1,32,256]{4,3,2,1,0:T(8,128)S(1)}, u32[]{:S(2)}, u32[]{:S(2)}) collective-permute-start(f32[2,1,1,32,256]{4,3,2,1,0:T(8,128)S(1)} %get-tuple-element.643), channel_id=1, source_target_pairs={{1,0},{2,1},{3,2},{4,3},{5,4},{6,5},{7,6},{9,8},{10,9},{11,10},{12... | collective-permute-start | bytes 196616 | tf_op jit(solution)/shard_map/while/body/eval_jaxpr/ppermute | solution.py:21
  174.9 7.6 %collective-permute-start.1 = (f32[2,1,1,32,256]{4,3,2,1,0:T(8,128)S(1)}, f32[2,1,1,32,256]{4,3,2,1,0:T(8,128)S(1)}, u32[]{:S(2)}, u32[]{:S(2)}) collective-permute-start(f32[2,1,1,32,256]{4,3,2,1,0:T(8,128)S(1)} %get-tuple-element.644), channel_id=1, source_target_pairs={{0,1},{1,2},{2,3},{3,4},{4,5},{5,6},{6,7},{8,9},{9,10},{10,11},{11... | collective-permute-start | bytes 196616 | tf_op jit(solution)/shard_map/while/body/eval_jaxpr/ppermute | solution.py:19
  184.0 6.8 %collective-permute-start.2 = (f32[1,1,32,256]{3,2,1,0:T(8,128)S(1)}, f32[1,1,32,256]{3,2,1,0:T(8,128)S(1)}, u32[]{:S(2)}, u32[]{:S(2)}) collective-permute-start(f32[1,1,32,256]{3,2,1,0:T(8,128)S(1)} %get-tuple-element.655), channel_id=1, source_target_pairs={{1,0},{2,1},{3,2},{4,3},{5,4},{6,5},{7,6},{9,8},{10,9},{11,10},{12... | collective-permute-start | bytes 98312 | tf_op jit(solution)/shard_map/while/body/eval_jaxpr/ppermute | solution.py:21
  185.3 7.0 %collective-permute-start.3 = (f32[1,1,32,256]{3,2,1,0:T(8,128)S(1)}, f32[1,1,32,256]{3,2,1,0:T(8,128)S(1)}, u32[]{:S(2)}, u32[]{:S(2)}) collective-permute-start(f32[1,1,32,256]{3,2,1,0:T(8,128)S(1)} %get-tuple-element.656), channel_id=1, source_target_pairs={{0,1},{1,2},{2,3},{3,4},{4,5},{5,6},{6,7},{8,9},{9,10},{10,11},{11... | collective-permute-start | bytes 98312 | tf_op jit(solution)/shard_map/while/body/eval_jaxpr/ppermute | solution.py:19
  192.5 7.1 %collective-permute-start.4 = (f32[1,1,32,256]{3,2,1,0:T(8,128)S(1)}, f32[1,1,32,256]{3,2,1,0:T(8,128)S(1)}, u32[]{:S(2)}, u32[]{:S(2)}) collective-permute-start(f32[1,1,32,256]{3,2,1,0:T(8,128)S(1)} %get-tuple-element.657), channel_id=1, source_target_pairs={{1,0},{2,1},{3,2},{4,3},{5,4},{6,5},{7,6},{9,8},{10,9},{11,10},{12... | collective-permute-start | bytes 98312 | tf_op jit(solution)/shard_map/while/body/eval_jaxpr/ppermute | solution.py:21
  193.8 7.4 %collective-permute-start.5 = (f32[1,1,32,256]{3,2,1,0:T(8,128)S(1)}, f32[1,1,32,256]{3,2,1,0:T(8,128)S(1)}, u32[]{:S(2)}, u32[]{:S(2)}) collective-permute-start(f32[1,1,32,256]{3,2,1,0:T(8,128)S(1)} %get-tuple-element.658), channel_id=1, source_target_pairs={{0,1},{1,2},{2,3},{3,4},{4,5},{5,6},{6,7},{8,9},{9,10},{10,11},{11... | collective-permute-start | bytes 98312 | tf_op jit(solution)/shard_map/while/body/eval_jaxpr/ppermute | solution.py:19
  199.6 1.6 copy-start.3
  201.2 0.6 copy-start.4
  203.3 7.4 %copy-start.6 = (s32[32768]{0:T(1024)S(1)}, s32[32768]{0:T(1024)}, u32[]{:S(2)}) copy-start(s32[32768]{0:T(1024)} %get-tuple-element.719) | copy-start | bytes 393220 | tf_op jit(solution)/shard_map/while
  203.3 11.9 %collective-permute-start.6 = (f32[2,1,1,32,256]{4,3,2,1,0:T(8,128)S(1)}, f32[2,1,1,32,256]{4,3,2,1,0:T(8,128)S(1)}, u32[]{:S(2)}, u32[]{:S(2)}) collective-permute-start(f32[2,1,1,32,256]{4,3,2,1,0:T(8,128)S(1)} %get-tuple-element.661), channel_id=1, source_target_pairs={{1,0},{2,1},{3,2},{4,3},{5,4},{6,5},{7,6},{9,8},{10,9},{11,10},{12... | collective-permute-start | bytes 196616 | tf_op jit(solution)/shard_map/while/body/eval_jaxpr/ppermute | solution.py:21
  204.8 10.5 %collective-permute-start.7 = (f32[2,1,1,32,256]{4,3,2,1,0:T(8,128)S(1)}, f32[2,1,1,32,256]{4,3,2,1,0:T(8,128)S(1)}, u32[]{:S(2)}, u32[]{:S(2)}) collective-permute-start(f32[2,1,1,32,256]{4,3,2,1,0:T(8,128)S(1)} %get-tuple-element.662), channel_id=1, source_target_pairs={{0,1},{1,2},{2,3},{3,4},{4,5},{5,6},{6,7},{8,9},{9,10},{10,11},{11... | collective-permute-start | bytes 196616 | tf_op jit(solution)/shard_map/while/body/eval_jaxpr/ppermute | solution.py:19
  228.6 38.3 %all-to-all-start.2 = ((f32[4,1,4,32,256]{4,3,2,1,0:T(8,128)}), f32[4,1,4,32,256]{4,3,2,1,0:T(8,128)S(1)}, u32[]{:S(2)}, u32[]{:S(2)}) async-start(f32[4,1,4,32,256]{4,3,2,1,0:T(8,128)} %get-tuple-element.381), calls=%async_computation.2 | async-start | bytes 1048576 | tf_op jit(solution)/shard_map/all_to_all | solution.py:190
